TPU v7x, 32 devices: a whole 2x2x4 slice. The times are simulated.
32 devices in a mesh: group: 2 (over x), fsdp: 4 (over z), inner: 4 (over y, core).
Axes of the slice: x: 2, y: 2, z: 4, core: 2. Of those that a mesh axis runs over, the one named last changes fastest.
Arguments:
- query_latent: bfloat16 [64, 3, 1536], P(('group', 'inner')), may hold values from -12 to 12
- new_entries: bfloat16 [64, 3, 576], P(('group', 'inner')), may hold values from -6 to 6
- latent_cache: bfloat16 [64, 512, 576], P(('group', 'inner')), may hold values from -800 to 800
- lengths: int32 [64], P(('group', 'inner')), may hold values from 128 to 512
- query_up: float32 [1536, 1024], P(('group', 'inner'), 'fsdp'), may hold values from -0.15625 to 0.15625
- key_up: float32 [512, 1024], P(('group', 'inner'), 'fsdp'), may hold values from -0.25 to 0.25
- query_moment: float32 [1536, 1024], P(('group', 'inner'), 'fsdp'), may hold values from -3 to 3
- query_second: float32 [1536, 1024], P(('group', 'inner'), 'fsdp'), may hold values from 0.05 to 2
- key_moment: float32 [512, 1024], P(('group', 'inner'), 'fsdp'), may hold values from -3 to 3
- key_second: float32 [512, 1024], P(('group', 'inner'), 'fsdp'), may hold values from 0.05 to 2
- query_grads: bfloat16 [12288, 1024], P(('group', 'inner'), 'fsdp'), may hold values from -6 to 6
- key_grads: bfloat16 [4096, 1024], P(('group', 'inner'), 'fsdp'), may hold values from -6 to 6
- rope_query: bfloat16 [1536, 512], P(None, 'fsdp'), may hold values from -0.15625 to 0.15625
- value_up: bfloat16 [512, 1024], P(None, 'fsdp'), may hold values from -0.25 to 0.25
- output_weight: bfloat16 [1024, 7168], P('fsdp'), may hold values from -0.25 to 0.25
Outputs:
- query_weight: float32 [1536, 1024], P(('group', 'inner'), 'fsdp')
- key_weight: float32 [512, 1024], P(('group', 'inner'), 'fsdp')
- query_first: float32 [1536, 1024], P(('group', 'inner'), 'fsdp')
- query_square: float32 [1536, 1024], P(('group', 'inner'), 'fsdp')
- key_first: float32 [512, 1024], P(('group', 'inner'), 'fsdp')
- key_square: float32 [512, 1024], P(('group', 'inner'), 'fsdp')
- attended: bfloat16 [7168, 192], P('fsdp', ('group', 'inner'))
Inputs may be any that keep to these rules, and one draw needn't show every extreme that they name: `lengths`: each row's count of live cache slots; the new tokens follow them.
All inputs are finite; a program needn't handle non-finite values.
Results may differ from a plain program's by a relative error of at most 0.023.
Values may be sent and summed in bfloat16 or wider, within the bound.
No kernel may reach another device: no remote copies, remote signals or barrier semaphores. Data moves between devices by JAX's collectives and lax.ppermute only.
A program may use at most 64 MiB of HBM per device.

v0:
```python
import functools
import math

import jax
import jax.numpy as jnp
from jax import lax
from jax.experimental import pallas as pl
from jax.experimental.pallas import tpu as pltpu
from jax.sharding import PartitionSpec as P


QR = 1536
KL = 512
HD = 128
R = 64
STEPS = 3
CACHE = 512


first_decay = 0.9
second_decay = 0.95
adam_epsilon = 1e-08
weight_decay = 0.1
learn_rate = 0.003
step_count = 10
rope_base = 10000.0


def optimizer_step(weight, moment, second, gradient):
    moment = first_decay * moment + (1.0 - first_decay) * gradient
    second = second_decay * second + (1.0 - second_decay) * gradient * gradient
    first_fix = 1.0 - first_decay**step_count
    second_fix = 1.0 - second_decay**step_count
    update = moment / first_fix / (jnp.sqrt(second / second_fix) + adam_epsilon)
    return (weight - learn_rate * (update + weight_decay * weight), moment, second)


ROW_AXES = ("group", "inner")


def swap(value, axes, count, distance):
    return lax.ppermute(value, axes, [(i, i ^ distance) for i in range(count)])


def block(value, index, axis=0):
    return lax.dynamic_index_in_dim(value, index, axis, keepdims=False)


VMEM_SPEC = pl.BlockSpec(memory_space=pltpu.VMEM)
HBM_SPEC = pl.BlockSpec(memory_space=pltpu.HBM)


def in_hbm(value):
    return pltpu.with_memory_space_constraint(value, pltpu.HBM)


def place():
    me = lax.axis_index(ROW_AXES)
    return me // 2, me % 2, lax.axis_size(ROW_AXES) // 2


def rows_at(index, count):
    return pl.ds(pl.multiple_of(index * count, 16), count)


def own_kernel(query_own, key_own, latents, out, keep, give, sems):
    _, core, chips = place()
    copies = []
    for other in range(chips):
        start = 0
        for i, own in enumerate((query_own, key_own)):
            count = own.shape[0] // (2 * chips)
            copies.append(
                pltpu.make_async_copy(
                    own.at[rows_at(2 * other + core, count), :],
                    out.at[other, pl.ds(start, count), :],
                    sems.at[2 * other + i],
                )
            )
            start += count
    for copy in copies:
        copy.start()
    count = query_own.shape[0] // (2 * chips)
    values = latents[...].astype(jnp.float32)
    pad = jnp.zeros((values.shape[0], keep.shape[2] - count), jnp.float32)
    for other in range(chips):
        even, odd = (
            jnp.concatenate(
                [values[:, (2 * other + i) * count:(2 * other + i + 1) * count], pad], 1
            )
            for i in range(2)
        )
        keep[other] = jnp.where(core == 0, even, odd).astype(keep.dtype)
        give[other] = jnp.where(core == 0, odd, even).astype(give.dtype)
    for copy in copies:
        copy.wait()


def own_blocks(query_own, key_own, latents):
    chips = lax.axis_size(ROW_AXES) // 2
    width = query_own.shape[1]
    grad_rows = (query_own.shape[0] + key_own.shape[0]) // (2 * chips)
    return pl.pallas_call(
        own_kernel,
        out_shape=[jax.ShapeDtypeStruct((chips, grad_rows, width), query_own.dtype)]
        + [jax.ShapeDtypeStruct((chips, latents.shape[0], width), latents.dtype)] * 2,
        in_specs=[HBM_SPEC] * 2 + [VMEM_SPEC],
        out_specs=[VMEM_SPEC] * 3,
        scratch_shapes=[pltpu.SemaphoreType.DMA((2 * chips,))],
        compiler_params=pltpu.CompilerParams(vmem_limit_bytes=2 << 20),
        cost_estimate=pl.CostEstimate(flops=10**9, bytes_accessed=10**6, transcendentals=0),
        name="own",
    )(in_hbm(query_own), in_hbm(key_own), latents)


def pack_kernel(own, query_got, key_got, latent_own, latent_got, *outs):
    chip, core, chips = place()
    total, latent_out, packs = outs[0], outs[1], outs[2:]
    grad_rows = total.shape[0]
    for j in range(chips):
        other = chip ^ j
        start = 0
        for got in (query_got, key_got):
            count = got.shape[0] // (2 * chips)
            both = own[other, start:start + count, :].astype(jnp.float32)
            both = both + got[rows_at(2 * other + core, count), :].astype(jnp.float32)
            if j == 0:
                total[start:start + count, :] = both
            else:
                packs[j - 1][start:start + count, :] = both.astype(jnp.bfloat16)
            start += count
        latents = jnp.concatenate(
            [latent_own[other].astype(jnp.float32), latent_got[other].astype(jnp.float32)]
        ).astype(jnp.bfloat16)
        if j == 0:
            latent_out[...] = latents
        else:
            packs[j - 1][grad_rows:, :] = latents


def pack_sums(own, query_got, key_got, latent_own, latent_got):
    chips, grad_rows, width = own.shape
    tokens = latent_own.shape[1]
    total, latents, *packs = pl.pallas_call(
        pack_kernel,
        out_shape=[
            jax.ShapeDtypeStruct((grad_rows, width), jnp.float32),
            jax.ShapeDtypeStruct((2 * tokens, width), jnp.bfloat16),
        ]
        + [jax.ShapeDtypeStruct((grad_rows + 2 * tokens, width), jnp.bfloat16)] * (chips - 1),
        in_specs=[VMEM_SPEC] * 5,
        out_specs=[VMEM_SPEC] * (chips + 1),
        compiler_params=pltpu.CompilerParams(vmem_limit_bytes=8 << 20),
        cost_estimate=pl.CostEstimate(flops=10**9, bytes_accessed=10**6, transcendentals=0),
        name="pack",
    )(own, query_got, key_got, latent_own, latent_got)
    return total, latents, packs


def row_value(lengths, count, rows):
    token = lax.broadcasted_iota(jnp.int32, (count, rows), 0)
    row = lax.broadcasted_iota(jnp.int32, (count, rows), 1)
    return jnp.sum(jnp.where(token % rows == row, lengths, 0), 1, keepdims=True)


def rope_kernel(after, query, weight, entries, lengths, query_rope, new_keys):
    del after
    tokens, rows = query.shape[0], lengths.shape[1]
    half = R // 2
    step = lax.broadcasted_iota(jnp.int32, (tokens, 1), 0) // rows
    place_of = (row_value(lengths[...], tokens, rows) + step).astype(jnp.float32)
    index = lax.broadcasted_iota(jnp.int32, (tokens, half), 1).astype(jnp.float32)
    angles = place_of * jnp.exp(index * (-math.log(rope_base) / half))
    cosine, sine = jnp.cos(angles), jnp.sin(angles)

    def turn(vectors):
        first, second = vectors[:, :half], vectors[:, half:]
        return jnp.concatenate(
            [first * cosine - second * sine, first * sine + second * cosine], 1
        )

    projected = jnp.dot(query[...], weight[...], preferred_element_type=jnp.float32)
    heads = projected.shape[1] // R
    query_rope[...] = jnp.concatenate(
        [turn(projected[:, h * R:(h + 1) * R]) for h in range(heads)]
    ).astype(jnp.bfloat16)
    new_keys[:, :KL] = entries[:, :KL]
    new_keys[:, KL:] = turn(entries[:, KL:].astype(jnp.float32)).astype(jnp.bfloat16)


def rope(after, query, weight, entries, lengths):
    heads = weight.shape[1] // R
    return pl.pallas_call(
        rope_kernel,
        out_shape=[
            jax.ShapeDtypeStruct((heads * query.shape[0], R), jnp.bfloat16),
            jax.ShapeDtypeStruct(entries.shape, jnp.bfloat16),
        ],
        in_specs=[VMEM_SPEC] * 5,
        out_specs=[VMEM_SPEC] * 2,
        compiler_params=pltpu.CompilerParams(vmem_limit_bytes=4 << 20),
        name="rope",
    )(after, query, weight, entries, lengths)


def update_kernel(chips, *refs):
    total, latents = refs[:2]
    packs, refs = refs[2:chips + 1], refs[chips + 1:]
    states, outs = refs[:6], refs[6:]
    partial, gives = outs[6], outs[7:]
    grad_rows = total.shape[0]
    gradient = total[...]
    for got in packs:
        gradient = gradient + got[:grad_rows, :].astype(jnp.float32)
    start = 0
    halves = []
    for i in range(2):
        weight, moment, second = states[3 * i:3 * i + 3]
        count = weight.shape[0]
        new = optimizer_step(
            weight[...], moment[...], second[...], gradient[start:start + count]
        )
        for out, value in zip(outs[3 * i:3 * i + 3], new):
            out[...] = value
        halves.append(new[0].astype(jnp.bfloat16))
        start += count
    query_half, key_half = halves
    query_rows = query_half.shape[0]
    tokens = partial.shape[0]
    for j in range(chips):
        columns = latents[:, :query_rows] if j == 0 else packs[j - 1][grad_rows:, :query_rows]
        product = jnp.dot(columns, query_half, preferred_element_type=jnp.float32)
        if j == 0:
            partial[...] = product
        else:
            gives[j][:tokens, :] = product.astype(jnp.bfloat16)
            gives[j][tokens:, :] = key_half
    gives[0][...] = key_half


def update(total, latents, packs, states):
    chips = len(packs) + 1
    tokens, width = latents.shape
    key_rows = states[3].shape[0]
    *outs, = pl.pallas_call(
        functools.partial(update_kernel, chips),
        out_shape=[jax.ShapeDtypeStruct(x.shape, x.dtype) for x in states]
        + [
            jax.ShapeDtypeStruct((tokens, width), jnp.float32),
            jax.ShapeDtypeStruct((key_rows, width), jnp.bfloat16),
        ]
        + [jax.ShapeDtypeStruct((tokens + key_rows, width), jnp.bfloat16)] * (chips - 1),
        in_specs=[VMEM_SPEC] * (chips + 7),
        out_specs=[VMEM_SPEC] * (chips + 7),
        compiler_params=pltpu.CompilerParams(vmem_limit_bytes=8 << 20),
        cost_estimate=pl.CostEstimate(flops=4 * 10**9, bytes_accessed=10**6, transcendentals=0),
        name="update",
    )(total, latents, *packs, *states)
    return outs[:6], outs[6], outs[7], outs[8:]


def merge_kernel(partial, key_half, *refs):
    *gots, query_sum, pair = refs
    tokens = partial.shape[0] // 2
    key_rows = key_half.shape[0]
    total = partial[...]
    pair[:key_rows, :] = key_half[...]
    for j, got in enumerate(gots):
        total = total + got[:2 * tokens, :].astype(jnp.float32)
        pair[(j + 1) * key_rows:(j + 2) * key_rows, :] = got[2 * tokens:, :]
    query_sum[...] = total[:tokens]
    pair[(len(gots) + 1) * key_rows:, :] = total[tokens:].astype(jnp.bfloat16)


def merge(partial, key_half, gots):
    tokens, width = partial.shape
    rows = (len(gots) + 1) * key_half.shape[0] + tokens // 2
    return pl.pallas_call(
        merge_kernel,
        out_shape=[
            jax.ShapeDtypeStruct((tokens // 2, width), jnp.float32),
            jax.ShapeDtypeStruct((rows, width), jnp.bfloat16),
        ],
        in_specs=[VMEM_SPEC] * (len(gots) + 2),
        out_specs=[VMEM_SPEC] * 2,
        compiler_params=pltpu.CompilerParams(vmem_limit_bytes=2 << 20),
        name="merge",
    )(partial, key_half, *gots)


def attend_kernel(
    rows, shares, whole_out,
    query_sum, pair_own, pair_got, query_rope, new_keys, lengths, value_up, cache, weight,
    *outs,
):
    f32, bf16 = jnp.float32, jnp.bfloat16
    *outs, key_full = outs
    tokens = query_sum.shape[0]
    heads = query_sum.shape[1] // HD
    count = heads * tokens
    chip, core, chips = place()
    key_rows = KL // (2 * chips)
    for j in range(chips):
        for pair, side in ((pair_own, core), (pair_got, 1 - core)):
            at = rows_at(2 * (chip ^ j) + side, key_rows)
            key_full[at, :] = pair[j * key_rows:(j + 1) * key_rows, :]
    head_query = (query_sum[...] + pair_got[KL // 2:, :].astype(f32)).astype(bf16)
    nt = (((1,), (1,)), ((), ()))
    nn = (((1,), (0,)), ((), ()))

    def dot(a, b, dims):
        return lax.dot_general(a, b, dims, preferred_element_type=f32)

    latent_query = jnp.concatenate(
        [
            dot(head_query[:, h * HD:(h + 1) * HD], key_full[:, h * HD:(h + 1) * HD], nt)
            for h in range(heads)
        ]
    ).astype(bf16)
    rope = query_rope[...]
    scale = 1.0 / math.sqrt(HD + R)
    row_of = lax.broadcasted_iota(jnp.int32, (count, 1), 0)
    batch_of, step_of = row_of % rows, (row_of // rows) % STEPS
    scores = jnp.zeros((count, CACHE), f32)
    for b in range(rows):
        here = dot(latent_query, cache[b, :KL, :], nn) + dot(rope, cache[b, KL:, :], nn)
        scores = jnp.where(batch_of == b, here, scores)
    slot = lax.broadcasted_iota(jnp.int32, (count, CACHE), 1)
    scores = jnp.where(slot < row_value(lengths[...], count, rows), scores * scale, -jnp.inf)
    fresh = dot(latent_query, new_keys[:, :KL], nt) + dot(rope, new_keys[:, KL:], nt)
    key_at = lax.broadcasted_iota(jnp.int32, (count, tokens), 1)
    seen = (key_at % rows == batch_of) & (key_at // rows <= step_of)
    fresh = jnp.where(seen, fresh * scale, -jnp.inf)
    highest = jnp.maximum(
        jnp.max(scores, -1, keepdims=True), jnp.max(fresh, -1, keepdims=True)
    )
    scores, fresh = jnp.exp(scores - highest), jnp.exp(fresh - highest)
    denominator = jnp.sum(scores, -1, keepdims=True) + jnp.sum(fresh, -1, keepdims=True)
    probs = (scores / denominator).astype(bf16)
    latent_out = dot((fresh / denominator).astype(bf16), new_keys[:, :KL], nn)
    for b in range(rows):
        mine = jnp.where(batch_of == b, probs, jnp.zeros_like(probs))
        latent_out = latent_out + dot(mine, cache[b, :KL, :], nt)
    latent_out = latent_out.astype(bf16)
    head_values = jnp.concatenate(
        [
            dot(latent_out[h * tokens:(h + 1) * tokens], value_up[:, h * HD:(h + 1) * HD], nn)
            for h in range(heads)
        ],
        1,
    ).astype(bf16)
    into = lax.broadcasted_iota(jnp.int32, (tokens, tokens), 0)
    origin = lax.broadcasted_iota(jnp.int32, (tokens, tokens), 1)
    order = origin == (into % STEPS) * rows + into // STEPS
    order = jnp.where(order, 1.0, 0.0).astype(bf16)
    head_values = dot(order, head_values, nn).astype(bf16)
    if whole_out:
        outs[0][...] = dot(head_values, weight[...], nn)
        return
    share = lax.axis_index("fsdp")
    part = weight.shape[1] // shares
    for j in range(shares):
        columns = pl.ds(pl.multiple_of((share ^ j) * part, 128), part)
        outs[j][...] = dot(head_values, weight[:, columns], nn).astype(outs[j].dtype)


def attend(
    query_sum, pair_own, pair_got, query_rope, new_keys, lengths, value_up, cache, weight
):
    rows = lengths.shape[0]
    tokens, columns = rows * STEPS, weight.shape[1]
    width = query_sum.shape[1]
    shares = lax.axis_size("fsdp")
    part = columns // shares
    whole_out = part % 128 != 0
    if whole_out:
        outs = [jax.ShapeDtypeStruct((tokens, columns), jnp.float32)]
    else:
        outs = [
            jax.ShapeDtypeStruct((tokens, part), jnp.bfloat16 if j else jnp.float32)
            for j in range(shares)
        ]
    outs = pl.pallas_call(
        functools.partial(attend_kernel, rows, shares, whole_out),
        out_shape=outs,
        in_specs=[VMEM_SPEC] * 9,
        out_specs=[VMEM_SPEC] * len(outs),
        scratch_shapes=[pltpu.VMEM((KL, width), jnp.bfloat16)],
        compiler_params=pltpu.CompilerParams(vmem_limit_bytes=24 << 20),
        name="attend",
    )(
        query_sum, pair_own, pair_got, query_rope, new_keys, lengths[None, :],
        value_up, cache, weight,
    )
    if whole_out:
        share = lax.axis_index("fsdp")
        blocks = outs[0].reshape(tokens, shares, part)
        own = block(blocks, share, 1)
        blocks = blocks.astype(jnp.bfloat16)
        return [own] + [block(blocks, share ^ j, 1) for j in range(1, shares)]
    return outs


def per_device(
    query_latent,
    new_entries,
    latent_cache,
    lengths,
    query_up,
    key_up,
    query_moment,
    query_second,
    key_moment,
    key_second,
    query_grads,
    key_grads,
    rope_query,
    value_up,
    output_weight,
):
    _, _, chips = place()
    devices = 2 * chips
    row_count = query_latent.shape[0]
    tokens = row_count * STEPS
    flat_query = query_latent.transpose(1, 0, 2).reshape(tokens, QR)

    query_got = swap(query_grads, ROW_AXES, devices, 1)
    key_got = swap(key_grads, ROW_AXES, devices, 1)
    own, latent_keep, latent_give = own_blocks(query_grads, key_grads, flat_query)
    latent_got = swap(latent_give, ROW_AXES, devices, 1)
    total, columns, packs = pack_sums(own, query_got, key_got, latent_keep, latent_got)
    query_rope, new_keys = rope(
        columns,
        flat_query,
        rope_query,
        new_entries.transpose(1, 0, 2).reshape(tokens, KL + R),
        lengths[None, :],
    )
    packs = [swap(pack, ROW_AXES, devices, 2 * j + 2) for j, pack in enumerate(packs)]

    states = (query_up, query_moment, query_second, key_up, key_moment, key_second)
    states, query_sum, key_half, gives = update(total, columns, packs, states)
    query_weight, query_first, query_square, key_weight, key_first, key_square = states
    gots = [swap(give, ROW_AXES, devices, 2 * j + 2) for j, give in enumerate(gives)]
    query_sum, pair_own = merge(query_sum, key_half, gots)
    pair_got = swap(pair_own, ROW_AXES, devices, 1)
    cache, weight = latent_cache.transpose(0, 2, 1), output_weight
    attended, *give = attend(
        query_sum, pair_own, pair_got, query_rope, new_keys, lengths, value_up, cache, weight
    )
    shares = lax.axis_size("fsdp")
    packs = [swap(pack, "fsdp", shares, j + 1) for j, pack in enumerate(give)]
    for pack in packs:
        attended = attended + pack.astype(jnp.float32)
    attended = attended.astype(jnp.bfloat16).T
    return (query_weight, key_weight, query_first, query_square, key_first, key_square, attended)


def solution(mesh):
    return step(mesh)


def step(mesh):
    return jax.shard_map(
        per_device,
        mesh=mesh,
        in_specs=(
            P(("group", "inner"), None, None),
            P(("group", "inner"), None, None),
            P(("group", "inner"), None, None),
            P(("group", "inner")),
            P(("group", "inner"), "fsdp"),
            P(("group", "inner"), "fsdp"),
            P(("group", "inner"), "fsdp"),
            P(("group", "inner"), "fsdp"),
            P(("group", "inner"), "fsdp"),
            P(("group", "inner"), "fsdp"),
            P(("group", "inner"), "fsdp"),
            P(("group", "inner"), "fsdp"),
            P(None, "fsdp"),
            P(None, "fsdp"),
            P("fsdp", None),
        ),
        out_specs=(
            P(("group", "inner"), "fsdp"),
            P(("group", "inner"), "fsdp"),
            P(("group", "inner"), "fsdp"),
            P(("group", "inner"), "fsdp"),
            P(("group", "inner"), "fsdp"),
            P(("group", "inner"), "fsdp"),
            P("fsdp", ("group", "inner")),
        ),
        check_vma=False,
    )
```

profile of v0, /device:TPU:0, one launch (start us, length us, event | category | flops | bytes accessed | tf_op | source)
XLA Modules:
  0.0 43.5 jit_solution(3792871759407009849)
XLA Ops:
  0.6 0.6 %collective-permute-start = (bf16[1536,256]{1,0:T(8,128)(2,1)}, bf16[1536,256]{1,0:T(8,128)(2,1)S(1)}, u32[]{:S(2)}, u32[]{:S(2)}) collective-permute-start(bf16[1536,256]{1,0:T(8,128)(2,1)} %query_own.1), channel_id=1, source_target_pairs={{0,1},{1,0},{2,3},{3,2},{16,17},{17,16},{18,19},{19,18},{4,5},{5,4... | collective-permute-start | bytes 2359304 | tf_op jit(solution)/shard_map/ppermute | solution.py:42
  1.2 0.1 collective-permute-start.1
  1.3 0.0 copy-start.3
  1.3 0.9 %copy-done.3 = bf16[8,3,1536]{2,0,1:T(8,128)(2,1)S(1)} copy-done((bf16[8,3,1536]{2,0,1:T(8,128)(2,1)S(1)}, bf16[8,3,1536]{2,0,1:T(8,128)(2,1)}, u32[]{:S(2)}) %copy-start.3) | copy-done | bytes 73752
  2.2 0.0 copy-start.7
  2.2 0.0 copy-start.8
  2.2 0.0 copy-start.9
  2.2 0.0 copy-start.10
  2.2 0.0 copy-start.11
  2.2 0.0 copy-start.12
  2.2 1.2 %own.1 = (bf16[4,256,256]{2,1,0:T(8,128)(2,1)S(1)}, bf16[4,24,256]{2,1,0:T(8,128)(2,1)S(1)}, bf16[4,24,256]{2,1,0:T(8,128)(2,1)S(1)}) custom-call(bf16[1536,256]{1,0:T(8,128)(2,1)} %query_own.1, bf16[512,256]{1,0:T(8,128)(2,1)} %key_own.1, bf16[24,1536]{1,0:T(8,128)(2,1)S(1)} %bitcast.13), custom_call_target="tpu_custom_call" | custom-call | flops 1000000000 | bytes 1000000 | tf_op jit(solution)/shard_map/own/pallas_call | solution.py:103
  3.4 0.5 %collective-permute-start.2 = (bf16[4,24,256]{2,1,0:T(8,128)(2,1)S(1)}, bf16[4,24,256]{2,1,0:T(8,128)(2,1)S(1)}, u32[]{:S(2)}, u32[]{:S(2)}) collective-permute-start(bf16[4,24,256]{2,1,0:T(8,128)(2,1)S(1)} %get-tuple-element.36), channel_id=1, source_target_pairs={{0,1},{1,0},{2,3},{3,2},{16,17},{17,16},{18,19},{19,18},{4,5},{5,4... | collective-permute-start | bytes 147464 | tf_op jit(solution)/shard_map/ppermute | solution.py:42
  3.9 0.9 %collective-permute-done.2.latent_got = bf16[4,24,256]{2,1,0:T(8,128)(2,1)S(1)} collective-permute-done((bf16[4,24,256]{2,1,0:T(8,128)(2,1)S(1)}, bf16[4,24,256]{2,1,0:T(8,128)(2,1)S(1)}, u32[]{:S(2)}, u32[]{:S(2)}) %collective-permute-start.2) | collective-permute-done | bytes 49184 | tf_op jit(solution)/shard_map/ppermute | solution.py:42
  4.8 0.0 collective-permute-done.1.key_got
  4.8 0.0 collective-permute-done.query_got
  4.8 0.0 slice-start
  4.8 0.1 pack.1
  5.0 2.9 %collective-permute-start.3 = (bf16[304,256]{1,0:T(8,128)(2,1)S(1)}, bf16[304,256]{1,0:T(8,128)(2,1)S(1)}, u32[]{:S(2)}, u32[]{:S(2)}) collective-permute-start(bf16[304,256]{1,0:T(8,128)(2,1)S(1)} %get-tuple-element.39), channel_id=1, source_target_pairs={{0,2},{1,3},{2,0},{3,1},{16,18},{17,19},{18,16},{19,17},{4,6},{5,7... | collective-permute-start | bytes 466952 | tf_op jit(solution)/shard_map/ppermute | solution.py:42
  7.9 1.5 %collective-permute-start.4 = (bf16[304,256]{1,0:T(8,128)(2,1)S(1)}, bf16[304,256]{1,0:T(8,128)(2,1)S(1)}, u32[]{:S(2)}, u32[]{:S(2)}) collective-permute-start(bf16[304,256]{1,0:T(8,128)(2,1)S(1)} %get-tuple-element.40), channel_id=1, source_target_pairs={{0,16},{1,17},{2,18},{3,19},{16,0},{17,1},{18,2},{19,3},{4,20},{5,... | collective-permute-start | bytes 466952 | tf_op jit(solution)/shard_map/ppermute | solution.py:42
  9.4 0.0 collective-permute-start.5
  9.4 2.8 %collective-permute-done.3.refs_2_ = bf16[304,256]{1,0:T(8,128)(2,1)S(1)} collective-permute-done((bf16[304,256]{1,0:T(8,128)(2,1)S(1)}, bf16[304,256]{1,0:T(8,128)(2,1)S(1)}, u32[]{:S(2)}, u32[]{:S(2)}) %collective-permute-start.3) | collective-permute-done | bytes 155680 | tf_op jit(solution)/shard_map/ppermute | solution.py:42
  12.2 2.6 %collective-permute-done.4.refs_3_ = bf16[304,256]{1,0:T(8,128)(2,1)S(1)} collective-permute-done((bf16[304,256]{1,0:T(8,128)(2,1)S(1)}, bf16[304,256]{1,0:T(8,128)(2,1)S(1)}, u32[]{:S(2)}, u32[]{:S(2)}) %collective-permute-start.4) | collective-permute-done | bytes 155680 | tf_op jit(solution)/shard_map/ppermute | solution.py:42
  14.8 2.0 %collective-permute-done.5.refs_4_ = bf16[304,256]{1,0:T(8,128)(2,1)S(1)} collective-permute-done((bf16[304,256]{1,0:T(8,128)(2,1)S(1)}, bf16[304,256]{1,0:T(8,128)(2,1)S(1)}, u32[]{:S(2)}, u32[]{:S(2)}) %collective-permute-start.5) | collective-permute-done | bytes 155680 | tf_op jit(solution)/shard_map/ppermute | solution.py:42
  16.8 0.0 copy-done.7
  16.8 0.0 copy-done.8
  16.8 0.0 copy-done.9
  16.8 0.0 copy-done.10
  16.8 0.0 copy-done.11
  16.9 0.0 copy-done.12
  16.9 0.0 copy-start.1
  16.9 0.0 copy-start.4
  16.9 0.0 copy-start.5
  16.9 0.0 copy-start.6
  16.9 0.0 slice-start.1
  16.9 0.0 copy-start
  16.9 0.0 copy-start.2
  16.9 1.2 %update.1 = (f32[192,256]{1,0:T(8,128)}, f32[192,256]{1,0:T(8,128)}, f32[192,256]{1,0:T(8,128)}, f32[64,256]{1,0:T(8,128)}, f32[64,256]{1,0:T(8,128)}, /*index=5...) custom-call(f32[256,256]{1,0:T(8,128)S(1)} %get-tuple-element.37.ref, ...), custom_call_target="tpu_custom_call" | custom-call | flops 4000000000 | bytes 1000000 | tf_op jit(solution)/shard_map/update/pallas_call | solution.py:245
  18.1 1.7 %collective-permute-start.6 = (bf16[112,256]{1,0:T(8,128)(2,1)S(1)}, bf16[112,256]{1,0:T(8,128)(2,1)S(1)}, u32[]{:S(2)}, u32[]{:S(2)}) collective-permute-start(bf16[112,256]{1,0:T(8,128)(2,1)S(1)} %get-tuple-element.50), channel_id=1, source_target_pairs={{0,2},{1,3},{2,0},{3,1},{16,18},{17,19},{18,16},{19,17},{4,6},{5,7... | collective-permute-start | bytes 172040 | tf_op jit(solution)/shard_map/ppermute | solution.py:42
  19.8 1.5 %collective-permute-start.7 = (bf16[112,256]{1,0:T(8,128)(2,1)S(1)}, bf16[112,256]{1,0:T(8,128)(2,1)S(1)}, u32[]{:S(2)}, u32[]{:S(2)}) collective-permute-start(bf16[112,256]{1,0:T(8,128)(2,1)S(1)} %get-tuple-element.51), channel_id=1, source_target_pairs={{0,16},{1,17},{2,18},{3,19},{16,0},{17,1},{18,2},{19,3},{4,20},{5,... | collective-permute-start | bytes 172040 | tf_op jit(solution)/shard_map/ppermute | solution.py:42
  21.3 0.3 collective-permute-start.8
  21.6 0.7 %collective-permute-done.6.refs_0_ = bf16[112,256]{1,0:T(8,128)(2,1)S(1)} collective-permute-done((bf16[112,256]{1,0:T(8,128)(2,1)S(1)}, bf16[112,256]{1,0:T(8,128)(2,1)S(1)}, u32[]{:S(2)}, u32[]{:S(2)}) %collective-permute-start.6) | collective-permute-done | bytes 57376 | tf_op jit(solution)/shard_map/ppermute | solution.py:42
  22.3 1.7 %collective-permute-done.7.refs_1_ = bf16[112,256]{1,0:T(8,128)(2,1)S(1)} collective-permute-done((bf16[112,256]{1,0:T(8,128)(2,1)S(1)}, bf16[112,256]{1,0:T(8,128)(2,1)S(1)}, u32[]{:S(2)}, u32[]{:S(2)}) %collective-permute-start.7) | collective-permute-done | bytes 57376 | tf_op jit(solution)/shard_map/ppermute | solution.py:42
  24.0 2.4 %collective-permute-done.8.refs_2_ = bf16[112,256]{1,0:T(8,128)(2,1)S(1)} collective-permute-done((bf16[112,256]{1,0:T(8,128)(2,1)S(1)}, bf16[112,256]{1,0:T(8,128)(2,1)S(1)}, u32[]{:S(2)}, u32[]{:S(2)}) %collective-permute-start.8) | collective-permute-done | bytes 57376 | tf_op jit(solution)/shard_map/ppermute | solution.py:42
  26.4 0.1 collective-permute-start.9
  26.4 0.0 copy-done.1
  26.5 0.0 copy-done.4
  26.5 0.0 copy-done.5
  26.5 0.0 copy-done.6
  26.5 0.4 rope.1
  26.9 0.9 %collective-permute-done.9.pair_got = bf16[280,256]{1,0:T(8,128)(2,1)S(1)} collective-permute-done((bf16[280,256]{1,0:T(8,128)(2,1)S(1)}, bf16[280,256]{1,0:T(8,128)(2,1)S(1)}, u32[]{:S(2)}, u32[]{:S(2)}) %collective-permute-start.9) | collective-permute-done | bytes 143392 | tf_op jit(solution)/shard_map/ppermute | solution.py:42
  27.8 0.0 slice-done
  27.8 0.0 slice-done.1
  27.8 0.0 copy-done
  27.8 0.0 copy-done.2
  27.8 3.6 %attend.1 = (f32[24,1792]{1,0:T(8,128)S(1)}, bf16[24,1792]{1,0:T(8,128)(2,1)S(1)}, bf16[24,1792]{1,0:T(8,128)(2,1)S(1)}, bf16[24,1792]{1,0:T(8,128)(2,1)S(1)}) custom-call(f32[24,256]{1,0:T(8,128)S(1)} %get-tuple-element.53.query_sum, bf16[280,256]{1,0:T(8,128)(2,1)S(1)} %get-tuple-element.54.pair_own, bf16[280,256]{1,0:T(8,128)(2,1)S(1)} %collective-permute-done.9.pair_got, ...), custom_call_target="tpu_custom_call" | custom-call | tf_op jit(solution)/shard_map/attend/pallas_call | solution.py:383
  31.4 1.6 %collective-permute-start.10 = (bf16[24,1792]{1,0:T(8,128)(2,1)S(1)}, bf16[24,1792]{1,0:T(8,128)(2,1)S(1)}, u32[]{:S(2)}, u32[]{:S(2)}) collective-permute-start(bf16[24,1792]{1,0:T(8,128)(2,1)S(1)} %get-tuple-element.58), channel_id=1, source_target_pairs={{0,4},{4,0},{8,12},{12,8},{1,5},{5,1},{9,13},{13,9},{2,6},{6,2},{1... | collective-permute-start | bytes 258056 | tf_op jit(solution)/shard_map/ppermute | solution.py:42
  33.0 2.6 %collective-permute-start.11 = (bf16[24,1792]{1,0:T(8,128)(2,1)S(1)}, bf16[24,1792]{1,0:T(8,128)(2,1)S(1)}, u32[]{:S(2)}, u32[]{:S(2)}) collective-permute-start(bf16[24,1792]{1,0:T(8,128)(2,1)S(1)} %get-tuple-element.59), channel_id=1, source_target_pairs={{0,8},{4,12},{8,0},{12,4},{1,9},{5,13},{9,1},{13,5},{2,10},{6,14},... | collective-permute-start | bytes 258056 | tf_op jit(solution)/shard_map/ppermute | solution.py:42
  35.6 0.2 collective-permute-start.12
  35.8 0.2 collective-permute-done.10
  36.0 6.8 %collective-permute-done.11 = bf16[24,1792]{1,0:T(8,128)(2,1)S(1)} collective-permute-done((bf16[24,1792]{1,0:T(8,128)(2,1)S(1)}, bf16[24,1792]{1,0:T(8,128)(2,1)S(1)}, u32[]{:S(2)}, u32[]{:S(2)}) %collective-permute-start.11) | collective-permute-done | bytes 86048 | tf_op jit(solution)/shard_map/ppermute | solution.py:42
  42.8 0.0 collective-permute-done.12
  42.8 0.7 %fusion = bf16[1792,24]{0,1:T(8,128)(2,1)} fusion(bf16[24,1792]{1,0:T(8,128)(2,1)S(1)} %collective-permute-done.12, bf16[24,1792]{1,0:T(8,128)(2,1)S(1)} %collective-permute-done.11, f32[24,1792]{1,0:T(8,128)S(1)} %get-tuple-element.57, bf16[24,1792]{1,0:T(8,128)(2,1)S(1)} %collective-permute-done.10), kind=kLoop, calls=%fused_computation.1 | loop fusion | flops 301056 | bytes 516096 | tf_op jit(solution)/shard_map/transpose | solution.py:455
  (2 shorter events, 0.0 us)
Async XLA Ops:
  0.6 4.2 %collective-permute-start = (bf16[1536,256]{1,0:T(8,128)(2,1)}, bf16[1536,256]{1,0:T(8,128)(2,1)S(1)}, u32[]{:S(2)}, u32[]{:S(2)}) collective-permute-start(bf16[1536,256]{1,0:T(8,128)(2,1)} %query_own.1), channel_id=1, source_target_pairs={{0,1},{1,0},{2,3},{3,2},{16,17},{17,16},{18,19},{19,18},{4,5},{5,4... | collective-permute-start | bytes 2359304 | tf_op jit(solution)/shard_map/ppermute | solution.py:42
  1.2 3.6 %collective-permute-start.1 = (bf16[512,256]{1,0:T(8,128)(2,1)}, bf16[512,256]{1,0:T(8,128)(2,1)S(1)}, u32[]{:S(2)}, u32[]{:S(2)}) collective-permute-start(bf16[512,256]{1,0:T(8,128)(2,1)} %key_own.1), channel_id=1, source_target_pairs={{0,1},{1,0},{2,3},{3,2},{16,17},{17,16},{18,19},{19,18},{4,5},{5,4... | collective-permute-start | bytes 786440 | tf_op jit(solution)/shard_map/ppermute | solution.py:42
  1.3 0.9 %copy-start.3 = (bf16[8,3,1536]{2,0,1:T(8,128)(2,1)S(1)}, bf16[8,3,1536]{2,0,1:T(8,128)(2,1)}, u32[]{:S(2)}) copy-start(bf16[8,3,1536]{2,0,1:T(8,128)(2,1)} %param.15) | copy-start | bytes 221188
  2.2 14.7 %copy-start.7 = (f32[192,256]{1,0:T(8,128)S(1)}, f32[192,256]{1,0:T(8,128)}, u32[]{:S(2)}) copy-start(f32[192,256]{1,0:T(8,128)} %refs_5_.1) | copy-start | bytes 589828
  2.2 14.7 %copy-start.8 = (f32[192,256]{1,0:T(8,128)S(1)}, f32[192,256]{1,0:T(8,128)}, u32[]{:S(2)}) copy-start(f32[192,256]{1,0:T(8,128)} %refs_6_.1) | copy-start | bytes 589828
  2.2 14.7 %copy-start.9 = (f32[192,256]{1,0:T(8,128)S(1)}, f32[192,256]{1,0:T(8,128)}, u32[]{:S(2)}) copy-start(f32[192,256]{1,0:T(8,128)} %refs_7_.1) | copy-start | bytes 589828
  2.2 14.7 %copy-start.10 = (f32[64,256]{1,0:T(8,128)S(1)}, f32[64,256]{1,0:T(8,128)}, u32[]{:S(2)}) copy-start(f32[64,256]{1,0:T(8,128)} %refs_8_.1) | copy-start | bytes 196612
  2.2 14.7 %copy-start.11 = (f32[64,256]{1,0:T(8,128)S(1)}, f32[64,256]{1,0:T(8,128)}, u32[]{:S(2)}) copy-start(f32[64,256]{1,0:T(8,128)} %refs_9_.1) | copy-start | bytes 196612
  2.2 14.7 %copy-start.12 = (f32[64,256]{1,0:T(8,128)S(1)}, f32[64,256]{1,0:T(8,128)}, u32[]{:S(2)}) copy-start(f32[64,256]{1,0:T(8,128)} %refs_10_.1) | copy-start | bytes 196612
  3.4 1.4 %collective-permute-start.2 = (bf16[4,24,256]{2,1,0:T(8,128)(2,1)S(1)}, bf16[4,24,256]{2,1,0:T(8,128)(2,1)S(1)}, u32[]{:S(2)}, u32[]{:S(2)}) collective-permute-start(bf16[4,24,256]{2,1,0:T(8,128)(2,1)S(1)} %get-tuple-element.36), channel_id=1, source_target_pairs={{0,1},{1,0},{2,3},{3,2},{16,17},{17,16},{18,19},{19,18},{4,5},{5,4... | collective-permute-start | bytes 147464 | tf_op jit(solution)/shard_map/ppermute | solution.py:42
  4.8 23.0 %slice-start = ((s8[4718592]{0:T(1024)(128)(4,1)}), s8[4194304]{0:T(1024)(128)(4,1)S(1)}, s32[]{:S(2)}) async-start(s8[4718592]{0:T(1024)(128)(4,1)} %bitcast.10), calls=%async_computation | async-start | bytes 8388608
  5.0 7.3 %collective-permute-start.3 = (bf16[304,256]{1,0:T(8,128)(2,1)S(1)}, bf16[304,256]{1,0:T(8,128)(2,1)S(1)}, u32[]{:S(2)}, u32[]{:S(2)}) collective-permute-start(bf16[304,256]{1,0:T(8,128)(2,1)S(1)} %get-tuple-element.39), channel_id=1, source_target_pairs={{0,2},{1,3},{2,0},{3,1},{16,18},{17,19},{18,16},{19,17},{4,6},{5,7... | collective-permute-start | bytes 466952 | tf_op jit(solution)/shard_map/ppermute | solution.py:42
  7.9 6.9 %collective-permute-start.4 = (bf16[304,256]{1,0:T(8,128)(2,1)S(1)}, bf16[304,256]{1,0:T(8,128)(2,1)S(1)}, u32[]{:S(2)}, u32[]{:S(2)}) collective-permute-start(bf16[304,256]{1,0:T(8,128)(2,1)S(1)} %get-tuple-element.40), channel_id=1, source_target_pairs={{0,16},{1,17},{2,18},{3,19},{16,0},{17,1},{18,2},{19,3},{4,20},{5,... | collective-permute-start | bytes 466952 | tf_op jit(solution)/shard_map/ppermute | solution.py:42
  9.4 7.4 %collective-permute-start.5 = (bf16[304,256]{1,0:T(8,128)(2,1)S(1)}, bf16[304,256]{1,0:T(8,128)(2,1)S(1)}, u32[]{:S(2)}, u32[]{:S(2)}) collective-permute-start(bf16[304,256]{1,0:T(8,128)(2,1)S(1)} %get-tuple-element.41), channel_id=1, source_target_pairs={{0,18},{1,19},{2,16},{3,17},{16,2},{17,3},{18,0},{19,1},{4,22},{5,... | collective-permute-start | bytes 466952 | tf_op jit(solution)/shard_map/ppermute | solution.py:42
  16.9 9.6 %copy-start.1 = (bf16[1536,128]{1,0:T(8,128)(2,1)S(1)}, bf16[1536,128]{1,0:T(8,128)(2,1)}, u32[]{:S(2)}) copy-start(bf16[1536,128]{1,0:T(8,128)(2,1)} %weight.2) | copy-start | bytes 1179652
  16.9 9.6 %copy-start.4 = (bf16[8,3,1536]{2,0,1:T(8,128)(2,1)S(1)}, bf16[8,3,1536]{2,0,1:T(8,128)(2,1)}, u32[]{:S(2)}) copy-start(bf16[8,3,1536]{2,0,1:T(8,128)(2,1)} %param.15) | copy-start | bytes 221188
  16.9 9.6 %copy-start.5 = (bf16[8,3,576]{2,0,1:T(8,128)(2,1)S(1)}, bf16[8,3,576]{2,0,1:T(8,128)(2,1)}, u32[]{:S(2)}) copy-start(bf16[8,3,576]{2,0,1:T(8,128)(2,1)} %param.16) | copy-start | bytes 82948
  16.9 9.6 %copy-start.6 = (s32[8]{0:T(128)S(1)}, s32[8]{0:T(128)}, u32[]{:S(2)}) copy-start(s32[8]{0:T(128)} %param.18) | copy-start | bytes 100
  16.9 10.9 %slice-start.1 = ((s8[4718592]{0:T(1024)(128)(4,1)}), s8[524288]{0:T(1024)(128)(4,1)S(1)}, s32[]{:S(2)}) async-start(s8[4718592]{0:T(1024)(128)(4,1)} %bitcast.10), calls=%async_computation.1 | async-start | bytes 1048576
  16.9 10.9 %copy-start = (bf16[256,7168]{1,0:T(8,128)(2,1)S(1)}, bf16[256,7168]{1,0:T(8,128)(2,1)}, u32[]{:S(2)}) copy-start(bf16[256,7168]{1,0:T(8,128)(2,1)} %weight.3) | copy-start | bytes 11010052
  16.9 10.9 %copy-start.2 = (bf16[512,256]{1,0:T(8,128)(2,1)S(1)}, bf16[512,256]{1,0:T(8,128)(2,1)}, u32[]{:S(2)}) copy-start(bf16[512,256]{1,0:T(8,128)(2,1)} %value_up.1) | copy-start | bytes 786436
  18.1 4.2 %collective-permute-start.6 = (bf16[112,256]{1,0:T(8,128)(2,1)S(1)}, bf16[112,256]{1,0:T(8,128)(2,1)S(1)}, u32[]{:S(2)}, u32[]{:S(2)}) collective-permute-start(bf16[112,256]{1,0:T(8,128)(2,1)S(1)} %get-tuple-element.50), channel_id=1, source_target_pairs={{0,2},{1,3},{2,0},{3,1},{16,18},{17,19},{18,16},{19,17},{4,6},{5,7... | collective-permute-start | bytes 172040 | tf_op jit(solution)/shard_map/ppermute | solution.py:42
  19.8 4.2 %collective-permute-start.7 = (bf16[112,256]{1,0:T(8,128)(2,1)S(1)}, bf16[112,256]{1,0:T(8,128)(2,1)S(1)}, u32[]{:S(2)}, u32[]{:S(2)}) collective-permute-start(bf16[112,256]{1,0:T(8,128)(2,1)S(1)} %get-tuple-element.51), channel_id=1, source_target_pairs={{0,16},{1,17},{2,18},{3,19},{16,0},{17,1},{18,2},{19,3},{4,20},{5,... | collective-permute-start | bytes 172040 | tf_op jit(solution)/shard_map/ppermute | solution.py:42
  21.3 5.1 %collective-permute-start.8 = (bf16[112,256]{1,0:T(8,128)(2,1)S(1)}, bf16[112,256]{1,0:T(8,128)(2,1)S(1)}, u32[]{:S(2)}, u32[]{:S(2)}) collective-permute-start(bf16[112,256]{1,0:T(8,128)(2,1)S(1)} %get-tuple-element.52), channel_id=1, source_target_pairs={{0,18},{1,19},{2,16},{3,17},{16,2},{17,3},{18,0},{19,1},{4,22},{5,... | collective-permute-start | bytes 172040 | tf_op jit(solution)/shard_map/ppermute | solution.py:42
  26.4 1.4 %collective-permute-start.9 = (bf16[280,256]{1,0:T(8,128)(2,1)S(1)}, bf16[280,256]{1,0:T(8,128)(2,1)S(1)}, u32[]{:S(2)}, u32[]{:S(2)}) collective-permute-start(bf16[280,256]{1,0:T(8,128)(2,1)S(1)} %get-tuple-element.54.pair_own), channel_id=1, source_target_pairs={{0,1},{1,0},{2,3},{3,2},{16,17},{17,16},{18,19},{19,18},{4,5},{5,4... | collective-permute-start | bytes 430088 | tf_op jit(solution)/shard_map/ppermute | solution.py:42
  31.4 4.6 %collective-permute-start.10 = (bf16[24,1792]{1,0:T(8,128)(2,1)S(1)}, bf16[24,1792]{1,0:T(8,128)(2,1)S(1)}, u32[]{:S(2)}, u32[]{:S(2)}) collective-permute-start(bf16[24,1792]{1,0:T(8,128)(2,1)S(1)} %get-tuple-element.58), channel_id=1, source_target_pairs={{0,4},{4,0},{8,12},{12,8},{1,5},{5,1},{9,13},{13,9},{2,6},{6,2},{1... | collective-permute-start | bytes 258056 | tf_op jit(solution)/shard_map/ppermute | solution.py:42
  33.0 9.8 %collective-permute-start.11 = (bf16[24,1792]{1,0:T(8,128)(2,1)S(1)}, bf16[24,1792]{1,0:T(8,128)(2,1)S(1)}, u32[]{:S(2)}, u32[]{:S(2)}) collective-permute-start(bf16[24,1792]{1,0:T(8,128)(2,1)S(1)} %get-tuple-element.59), channel_id=1, source_target_pairs={{0,8},{4,12},{8,0},{12,4},{1,9},{5,13},{9,1},{13,5},{2,10},{6,14},... | collective-permute-start | bytes 258056 | tf_op jit(solution)/shard_map/ppermute | solution.py:42
  35.6 7.2 %collective-permute-start.12 = (bf16[24,1792]{1,0:T(8,128)(2,1)S(1)}, bf16[24,1792]{1,0:T(8,128)(2,1)S(1)}, u32[]{:S(2)}, u32[]{:S(2)}) collective-permute-start(bf16[24,1792]{1,0:T(8,128)(2,1)S(1)} %get-tuple-element.60), channel_id=1, source_target_pairs={{0,12},{4,8},{8,4},{12,0},{1,13},{5,9},{9,5},{13,1},{2,14},{6,10},... | collective-permute-start | bytes 258056 | tf_op jit(solution)/shard_map/ppermute | solution.py:42
where the time goes:
time: 43.7 us; the launch traced here: 43.5 us
  waiting for transfers between devices  20.9 us (48%)
  starting transfers between devices  13.6 us (31%)
  Pallas kernels  6.49 us (15%)
  local copies, waits for them, and re-layouts  0.96 us (2%)
  between operations  0.83 us (2%)
  other arithmetic  0.69 us (2%)
    ppermute x13, waiting for transfers between devices, swap(): return lax.ppermute(value, axes, [(i, i ^ distance) for i in range(count)])  20.9 us
    ppermute x13, starting transfers between devices, swap(): return lax.ppermute(value, axes, [(i, i ^ distance) for i in range(count)])  13.6 us
    pallas_call x1, Pallas kernels, attend(): pl.pallas_call(functools.partial(attend_kernel, rows, shares, whole_out),...  3.56 us
    pallas_call x1, Pallas kernels, own_blocks(): pl.pallas_call(own_kernel, out_shape=[jax.ShapeDtypeStruct((chips, grad_r...  1.24 us
    pallas_call x1, Pallas kernels, update(): pl.pallas_call(functools.partial(update_kernel, chips), out_shape=[jax.Sh...  1.16 us
    unnamed x30, local copies, waits for them, and re-layouts  0.96 us
  transfers between devices with their start and end apart: 13, of which 10 were waited for; matrix products, arithmetic and copies ran while one was open for 0% of the time, Pallas kernels for 4%

commit v1 on v0

--- a/solution.py
+++ b/solution.py
@@ -63,8 +63,10 @@
     return pl.ds(pl.multiple_of(index * count, 16), count)
 
 
-def own_kernel(query_own, key_own, latents, out, keep, give, sems):
+def own_kernel(query_own, key_own, latents_in, out, keep, give, latents, sems):
     _, core, chips = place()
+    fetch = pltpu.make_async_copy(latents_in, latents, sems.at[2 * chips])
+    fetch.start()
     copies = []
     for other in range(chips):
         start = 0
@@ -81,6 +83,7 @@
     for copy in copies:
         copy.start()
     count = query_own.shape[0] // (2 * chips)
+    fetch.wait()
     values = latents[...].astype(jnp.float32)
     pad = jnp.zeros((values.shape[0], keep.shape[2] - count), jnp.float32)
     for other in range(chips):
@@ -104,13 +107,16 @@
         own_kernel,
         out_shape=[jax.ShapeDtypeStruct((chips, grad_rows, width), query_own.dtype)]
         + [jax.ShapeDtypeStruct((chips, latents.shape[0], width), latents.dtype)] * 2,
-        in_specs=[HBM_SPEC] * 2 + [VMEM_SPEC],
+        in_specs=[HBM_SPEC] * 3,
         out_specs=[VMEM_SPEC] * 3,
-        scratch_shapes=[pltpu.SemaphoreType.DMA((2 * chips,))],
+        scratch_shapes=[
+            pltpu.VMEM(latents.shape, latents.dtype),
+            pltpu.SemaphoreType.DMA((2 * chips + 1,)),
+        ],
         compiler_params=pltpu.CompilerParams(vmem_limit_bytes=2 << 20),
         cost_estimate=pl.CostEstimate(flops=10**9, bytes_accessed=10**6, transcendentals=0),
         name="own",
-    )(in_hbm(query_own), in_hbm(key_own), latents)
+    )(in_hbm(query_own), in_hbm(key_own), in_hbm(latents))
 
 
 def pack_kernel(own, query_got, key_got, latent_own, latent_got, *outs):
@@ -244,7 +250,7 @@
     key_rows = states[3].shape[0]
     *outs, = pl.pallas_call(
         functools.partial(update_kernel, chips),
-        out_shape=[jax.ShapeDtypeStruct(x.shape, x.dtype) for x in states]
+        out_shape=[pltpu.VMEM(x.shape, x.dtype) for x in states]
         + [
             jax.ShapeDtypeStruct((tokens, width), jnp.float32),
             jax.ShapeDtypeStruct((key_rows, width), jnp.bfloat16),
@@ -289,12 +295,11 @@
 
 
 def attend_kernel(
-    rows, shares, whole_out,
-    query_sum, pair_own, pair_got, query_rope, new_keys, lengths, value_up, cache, weight,
-    *outs,
+    rows,
+    query_sum, pair_own, pair_got, query_rope, new_keys, lengths, value_up, cache,
+    out, key_full,
 ):
     f32, bf16 = jnp.float32, jnp.bfloat16
-    *outs, key_full = outs
     tokens = query_sum.shape[0]
     heads = query_sum.shape[1] // HD
     count = heads * tokens
@@ -353,52 +358,60 @@
     origin = lax.broadcasted_iota(jnp.int32, (tokens, tokens), 1)
     order = origin == (into % STEPS) * rows + into // STEPS
     order = jnp.where(order, 1.0, 0.0).astype(bf16)
-    head_values = dot(order, head_values, nn).astype(bf16)
-    if whole_out:
-        outs[0][...] = dot(head_values, weight[...], nn)
-        return
-    share = lax.axis_index("fsdp")
-    part = weight.shape[1] // shares
-    for j in range(shares):
-        columns = pl.ds(pl.multiple_of((share ^ j) * part, 128), part)
-        outs[j][...] = dot(head_values, weight[:, columns], nn).astype(outs[j].dtype)
-
-
-def attend(
-    query_sum, pair_own, pair_got, query_rope, new_keys, lengths, value_up, cache, weight
-):
-    rows = lengths.shape[0]
-    tokens, columns = rows * STEPS, weight.shape[1]
-    width = query_sum.shape[1]
+    out[...] = dot(order, head_values, nn).astype(bf16)
+
+
+def attend(query_sum, pair_own, pair_got, query_rope, new_keys, lengths, value_up, cache):
+    tokens, width = query_sum.shape
+    return pl.pallas_call(
+        functools.partial(attend_kernel, lengths.shape[0]),
+        out_shape=jax.ShapeDtypeStruct((tokens, width), jnp.bfloat16),
+        in_specs=[VMEM_SPEC] * 8,
+        out_specs=VMEM_SPEC,
+        scratch_shapes=[pltpu.VMEM((KL, width), jnp.bfloat16)],
+        compiler_params=pltpu.CompilerParams(vmem_limit_bytes=16 << 20),
+        name="attend",
+    )(query_sum, pair_own, pair_got, query_rope, new_keys, lengths[None, :], value_up, cache)
+
+
+def project_kernel(distance, head_values, weight, out):
+    part = out.shape[1]
+    if part == weight.shape[1]:
+        columns = weight[...]
+    else:
+        share = lax.axis_index("fsdp")
+        columns = weight[:, pl.ds(pl.multiple_of((share ^ distance) * part, 128), part)]
+    out[...] = jnp.dot(
+        head_values[...], columns, preferred_element_type=jnp.float32
+    ).astype(out.dtype)
+
+
+def project(head_values, weight, distance, part, dtype):
+    return pl.pallas_call(
+        functools.partial(project_kernel, distance),
+        out_shape=jax.ShapeDtypeStruct((head_values.shape[0], part), dtype),
+        in_specs=[VMEM_SPEC] * 2,
+        out_specs=VMEM_SPEC,
+        compiler_params=pltpu.CompilerParams(vmem_limit_bytes=8 << 20),
+        name="project",
+    )(head_values, weight)
+
+
+def project_all(head_values, weight):
     shares = lax.axis_size("fsdp")
+    columns = weight.shape[1]
     part = columns // shares
-    whole_out = part % 128 != 0
-    if whole_out:
-        outs = [jax.ShapeDtypeStruct((tokens, columns), jnp.float32)]
-    else:
-        outs = [
-            jax.ShapeDtypeStruct((tokens, part), jnp.bfloat16 if j else jnp.float32)
+    if part % 128 == 0:
+        return [
+            project(head_values, weight, j, part, jnp.bfloat16 if j else jnp.float32)
             for j in range(shares)
         ]
-    outs = pl.pallas_call(
-        functools.partial(attend_kernel, rows, shares, whole_out),
-        out_shape=outs,
-        in_specs=[VMEM_SPEC] * 9,
-        out_specs=[VMEM_SPEC] * len(outs),
-        scratch_shapes=[pltpu.VMEM((KL, width), jnp.bfloat16)],
-        compiler_params=pltpu.CompilerParams(vmem_limit_bytes=24 << 20),
-        name="attend",
-    )(
-        query_sum, pair_own, pair_got, query_rope, new_keys, lengths[None, :],
-        value_up, cache, weight,
-    )
-    if whole_out:
-        share = lax.axis_index("fsdp")
-        blocks = outs[0].reshape(tokens, shares, part)
-        own = block(blocks, share, 1)
-        blocks = blocks.astype(jnp.bfloat16)
-        return [own] + [block(blocks, share ^ j, 1) for j in range(1, shares)]
-    return outs
+    whole = project(head_values, weight, 0, columns, jnp.float32)
+    share = lax.axis_index("fsdp")
+    blocks = whole.reshape(-1, shares, part)
+    own = block(blocks, share, 1)
+    blocks = blocks.astype(jnp.bfloat16)
+    return [own] + [block(blocks, share ^ j, 1) for j in range(1, shares)]
 
 
 def per_device(
@@ -444,10 +457,11 @@
     gots = [swap(give, ROW_AXES, devices, 2 * j + 2) for j, give in enumerate(gives)]
     query_sum, pair_own = merge(query_sum, key_half, gots)
     pair_got = swap(pair_own, ROW_AXES, devices, 1)
-    cache, weight = latent_cache.transpose(0, 2, 1), output_weight
-    attended, *give = attend(
-        query_sum, pair_own, pair_got, query_rope, new_keys, lengths, value_up, cache, weight
+    head_values = attend(
+        query_sum, pair_own, pair_got, query_rope, new_keys, lengths, value_up,
+        latent_cache.transpose(0, 2, 1),
     )
+    attended, *give = project_all(head_values, output_weight)
     shares = lax.axis_size("fsdp")
     packs = [swap(pack, "fsdp", shares, j + 1) for j, pack in enumerate(give)]
     for pack in packs:

time: 43.7 us -> 42.1 us (0.963)
  waiting for transfers between devices: 20.9 us -> 16.7 us
  local copies, waits for them, and re-layouts: 0.96 us -> 3.99 us
    ppermute x13, waiting for transfers between devices: 20.9 us -> 16.7 us  [swap(): return lax.ppermute(value, axes, [(i, i ^ distance) for i in range(count)])]
    unnamed x30 -> x34, local copies, waits for them, and re-layouts: 0.96 us -> 3.99 us
    pallas_call x2 -> x6, Pallas kernels: 4.72 us -> 4.38 us  [the longest x1 2.86 us: attend(): pl.pallas_call(functools.partial(attend_kernel, lengths.shape[0]), out_sh...]
  transfers between devices with their start and end apart: 13 -> 13, of which waited for: 10 -> 9; matrix products, arithmetic and copies ran while one was open for 0% -> 9% of each run, Pallas kernels for 4% -> 4%
where the time goes in v1:
time: 42.1 us; the launch traced here: 42 us
  waiting for transfers between devices  16.7 us (40%)
  starting transfers between devices  13.6 us (32%)
  Pallas kernels  6.11 us (15%)
  local copies, waits for them, and re-layouts  3.99 us (9%)
  between operations  0.85 us (2%)
  other arithmetic  0.69 us (2%)
    ppermute x13, waiting for transfers between devices, swap(): return lax.ppermute(value, axes, [(i, i ^ distance) for i in range(count)])  16.7 us
    ppermute x13, starting transfers between devices, swap(): return lax.ppermute(value, axes, [(i, i ^ distance) for i in range(count)])  13.6 us
    unnamed x34, local copies, waits for them, and re-layouts  3.99 us
    pallas_call x1, Pallas kernels, attend(): pl.pallas_call(functools.partial(attend_kernel, lengths.shape[0]), out_sh...  2.86 us
    pallas_call x1, Pallas kernels, own_blocks(): pl.pallas_call(own_kernel, out_shape=[jax.ShapeDtypeStruct((chips, grad_r...  1.2 us
    pallas_call x4, Pallas kernels, project(): pl.pallas_call(functools.partial(project_kernel, distance), out_shape=jax...  1.14 us
  transfers between devices with their start and end apart: 13, of which 9 were waited for; matrix products, arithmetic and copies ran while one was open for 9% of the time, Pallas kernels for 4%

profile of v1, /device:TPU:0, one launch (start us, length us, event | category | flops | bytes accessed | tf_op | source)
XLA Modules:
  0.0 42.0 jit_solution(12912192130161385571)
XLA Ops:
  0.6 0.0 copy-start.11
  0.6 0.0 copy-start.10
  0.7 0.0 copy-start.8
  0.7 0.0 copy-start.7
  0.7 0.0 copy-start.9
  0.7 0.0 copy-start.6
  0.7 0.6 %collective-permute-start = (bf16[1536,256]{1,0:T(8,128)(2,1)}, bf16[1536,256]{1,0:T(8,128)(2,1)S(1)}, u32[]{:S(2)}, u32[]{:S(2)}) collective-permute-start(bf16[1536,256]{1,0:T(8,128)(2,1)} %query_own.1), channel_id=1, source_target_pairs={{0,1},{1,0},{2,3},{3,2},{16,17},{17,16},{18,19},{19,18},{4,5},{5,4... | collective-permute-start | bytes 2359304 | tf_op jit(solution)/shard_map/ppermute | solution.py:42
  1.3 0.1 collective-permute-start.1
  1.3 1.2 %own.1 = (bf16[4,256,256]{2,1,0:T(8,128)(2,1)S(1)}, bf16[4,24,256]{2,1,0:T(8,128)(2,1)S(1)}, bf16[4,24,256]{2,1,0:T(8,128)(2,1)S(1)}) custom-call(bf16[1536,256]{1,0:T(8,128)(2,1)} %query_own.1, bf16[512,256]{1,0:T(8,128)(2,1)} %key_own.1, bf16[24,1536]{1,0:T(8,128)(2,1)} %bitcast.13), custom_call_target="tpu_custom_call" | custom-call | flops 1000000000 | bytes 1000000 | tf_op jit(solution)/shard_map/own/pallas_call | solution.py:106
  2.5 0.5 %collective-permute-start.2 = (bf16[4,24,256]{2,1,0:T(8,128)(2,1)S(1)}, bf16[4,24,256]{2,1,0:T(8,128)(2,1)S(1)}, u32[]{:S(2)}, u32[]{:S(2)}) collective-permute-start(bf16[4,24,256]{2,1,0:T(8,128)(2,1)S(1)} %get-tuple-element.32), channel_id=1, source_target_pairs={{0,1},{1,0},{2,3},{3,2},{16,17},{17,16},{18,19},{19,18},{4,5},{5,4... | collective-permute-start | bytes 147464 | tf_op jit(solution)/shard_map/ppermute | solution.py:42
  3.0 0.9 %collective-permute-done.2.latent_got = bf16[4,24,256]{2,1,0:T(8,128)(2,1)S(1)} collective-permute-done((bf16[4,24,256]{2,1,0:T(8,128)(2,1)S(1)}, bf16[4,24,256]{2,1,0:T(8,128)(2,1)S(1)}, u32[]{:S(2)}, u32[]{:S(2)}) %collective-permute-start.2) | collective-permute-done | bytes 49184 | tf_op jit(solution)/shard_map/ppermute | solution.py:42
  3.9 0.0 collective-permute-done.1.key_got
  3.9 0.0 collective-permute-done.query_got
  3.9 0.1 pack.1
  4.1 2.9 %collective-permute-start.3 = (bf16[304,256]{1,0:T(8,128)(2,1)S(1)}, bf16[304,256]{1,0:T(8,128)(2,1)S(1)}, u32[]{:S(2)}, u32[]{:S(2)}) collective-permute-start(bf16[304,256]{1,0:T(8,128)(2,1)S(1)} %get-tuple-element.35), channel_id=1, source_target_pairs={{0,2},{1,3},{2,0},{3,1},{16,18},{17,19},{18,16},{19,17},{4,6},{5,7... | collective-permute-start | bytes 466952 | tf_op jit(solution)/shard_map/ppermute | solution.py:42
  7.0 1.5 %collective-permute-start.4 = (bf16[304,256]{1,0:T(8,128)(2,1)S(1)}, bf16[304,256]{1,0:T(8,128)(2,1)S(1)}, u32[]{:S(2)}, u32[]{:S(2)}) collective-permute-start(bf16[304,256]{1,0:T(8,128)(2,1)S(1)} %get-tuple-element.36), channel_id=1, source_target_pairs={{0,16},{1,17},{2,18},{3,19},{16,0},{17,1},{18,2},{19,3},{4,20},{5,... | collective-permute-start | bytes 466952 | tf_op jit(solution)/shard_map/ppermute | solution.py:42
  8.5 0.0 collective-permute-start.5
  8.5 2.8 %collective-permute-done.3.refs_2_ = bf16[304,256]{1,0:T(8,128)(2,1)S(1)} collective-permute-done((bf16[304,256]{1,0:T(8,128)(2,1)S(1)}, bf16[304,256]{1,0:T(8,128)(2,1)S(1)}, u32[]{:S(2)}, u32[]{:S(2)}) %collective-permute-start.3) | collective-permute-done | bytes 155680 | tf_op jit(solution)/shard_map/ppermute | solution.py:42
  11.3 2.6 %collective-permute-done.4.refs_3_ = bf16[304,256]{1,0:T(8,128)(2,1)S(1)} collective-permute-done((bf16[304,256]{1,0:T(8,128)(2,1)S(1)}, bf16[304,256]{1,0:T(8,128)(2,1)S(1)}, u32[]{:S(2)}, u32[]{:S(2)}) %collective-permute-start.4) | collective-permute-done | bytes 155680 | tf_op jit(solution)/shard_map/ppermute | solution.py:42
  13.9 2.0 %collective-permute-done.5.refs_4_ = bf16[304,256]{1,0:T(8,128)(2,1)S(1)} collective-permute-done((bf16[304,256]{1,0:T(8,128)(2,1)S(1)}, bf16[304,256]{1,0:T(8,128)(2,1)S(1)}, u32[]{:S(2)}, u32[]{:S(2)}) %collective-permute-start.5) | collective-permute-done | bytes 155680 | tf_op jit(solution)/shard_map/ppermute | solution.py:42
  15.9 0.0 copy-done.11
  15.9 0.0 copy-done.10
  15.9 0.0 copy-done.8
  15.9 0.0 copy-done.7
  15.9 0.0 copy-done.9
  16.0 0.0 copy-done.6
  16.0 0.0 copy-start.1
  16.0 0.0 copy-start.3
  16.0 0.0 copy-start.4
  16.0 0.0 copy-start.5
  16.0 0.0 slice-start.1
  16.0 0.0 copy-start.2
  16.0 0.4 update.1
  16.4 1.7 %collective-permute-start.6 = (bf16[112,256]{1,0:T(8,128)(2,1)S(1)}, bf16[112,256]{1,0:T(8,128)(2,1)S(1)}, u32[]{:S(2)}, u32[]{:S(2)}) collective-permute-start(bf16[112,256]{1,0:T(8,128)(2,1)S(1)} %get-tuple-element.46), channel_id=1, source_target_pairs={{0,2},{1,3},{2,0},{3,1},{16,18},{17,19},{18,16},{19,17},{4,6},{5,7... | collective-permute-start | bytes 172040 | tf_op jit(solution)/shard_map/ppermute | solution.py:42
  18.2 1.5 %collective-permute-start.7 = (bf16[112,256]{1,0:T(8,128)(2,1)S(1)}, bf16[112,256]{1,0:T(8,128)(2,1)S(1)}, u32[]{:S(2)}, u32[]{:S(2)}) collective-permute-start(bf16[112,256]{1,0:T(8,128)(2,1)S(1)} %get-tuple-element.47), channel_id=1, source_target_pairs={{0,16},{1,17},{2,18},{3,19},{16,0},{17,1},{18,2},{19,3},{4,20},{5,... | collective-permute-start | bytes 172040 | tf_op jit(solution)/shard_map/ppermute | solution.py:42
  19.6 0.3 collective-permute-start.8
  20.0 0.7 %collective-permute-done.6.refs_0_ = bf16[112,256]{1,0:T(8,128)(2,1)S(1)} collective-permute-done((bf16[112,256]{1,0:T(8,128)(2,1)S(1)}, bf16[112,256]{1,0:T(8,128)(2,1)S(1)}, u32[]{:S(2)}, u32[]{:S(2)}) %collective-permute-start.6) | collective-permute-done | bytes 57376 | tf_op jit(solution)/shard_map/ppermute | solution.py:42
  20.7 1.7 %collective-permute-done.7.refs_1_ = bf16[112,256]{1,0:T(8,128)(2,1)S(1)} collective-permute-done((bf16[112,256]{1,0:T(8,128)(2,1)S(1)}, bf16[112,256]{1,0:T(8,128)(2,1)S(1)}, u32[]{:S(2)}, u32[]{:S(2)}) %collective-permute-start.7) | collective-permute-done | bytes 57376 | tf_op jit(solution)/shard_map/ppermute | solution.py:42
  22.3 2.4 %collective-permute-done.8.refs_2_ = bf16[112,256]{1,0:T(8,128)(2,1)S(1)} collective-permute-done((bf16[112,256]{1,0:T(8,128)(2,1)S(1)}, bf16[112,256]{1,0:T(8,128)(2,1)S(1)}, u32[]{:S(2)}, u32[]{:S(2)}) %collective-permute-start.8) | collective-permute-done | bytes 57376 | tf_op jit(solution)/shard_map/ppermute | solution.py:42
  24.8 0.1 collective-permute-start.9
  24.8 0.0 copy-done.1
  24.8 0.0 copy-done.3
  24.9 0.0 copy-done.4
  24.9 0.0 copy-done.5
  24.9 0.4 rope.1
  25.2 0.9 %collective-permute-done.9.pair_got = bf16[280,256]{1,0:T(8,128)(2,1)S(1)} collective-permute-done((bf16[280,256]{1,0:T(8,128)(2,1)S(1)}, bf16[280,256]{1,0:T(8,128)(2,1)S(1)}, u32[]{:S(2)}, u32[]{:S(2)}) %collective-permute-start.9) | collective-permute-done | bytes 143392 | tf_op jit(solution)/shard_map/ppermute | solution.py:42
  26.2 2.9 %attend.1.head_values = bf16[24,256]{1,0:T(8,128)(2,1)S(1)} custom-call(f32[24,256]{1,0:T(8,128)S(1)} %get-tuple-element.49.query_sum, bf16[280,256]{1,0:T(8,128)(2,1)S(1)} %get-tuple-element.50.pair_own, bf16[280,256]{1,0:T(8,128)(2,1)S(1)} %collective-permute-done.9.pair_got, bf16[48,64]{1,0:T(8,128)(2,1)S(1)} %get-tuple-element.51.query_rope, ...), custom_call_target="tpu_custom_call" | custom-call | tf_op jit(solution)/shard_map/attend/pallas_call | solution.py:366
  29.1 0.3 project.7
  29.4 0.3 project.6
  29.6 0.3 project.5
  29.9 1.6 %collective-permute-start.10 = (bf16[24,1792]{1,0:T(8,128)(2,1)S(1)}, bf16[24,1792]{1,0:T(8,128)(2,1)S(1)}, u32[]{:S(2)}, u32[]{:S(2)}) collective-permute-start(bf16[24,1792]{1,0:T(8,128)(2,1)S(1)} %project.5), channel_id=1, source_target_pairs={{0,4},{4,0},{8,12},{12,8},{1,5},{5,1},{9,13},{13,9},{2,6},{6,2},{1... | collective-permute-start | bytes 258056 | tf_op jit(solution)/shard_map/ppermute | solution.py:42
  31.5 2.6 %collective-permute-start.11 = (bf16[24,1792]{1,0:T(8,128)(2,1)S(1)}, bf16[24,1792]{1,0:T(8,128)(2,1)S(1)}, u32[]{:S(2)}, u32[]{:S(2)}) collective-permute-start(bf16[24,1792]{1,0:T(8,128)(2,1)S(1)} %project.6), channel_id=1, source_target_pairs={{0,8},{4,12},{8,0},{12,4},{1,9},{5,13},{9,1},{13,5},{2,10},{6,14},... | collective-permute-start | bytes 258056 | tf_op jit(solution)/shard_map/ppermute | solution.py:42
  34.1 0.2 collective-permute-start.12
  34.4 0.7 %copy.22 = f32[192,256]{1,0:T(8,128)} copy(f32[192,256]{1,0:T(8,128)S(1)} %get-tuple-element.53) | data formatting | bytes 393216
  35.0 0.6 %copy.23 = f32[64,256]{1,0:T(8,128)} copy(f32[64,256]{1,0:T(8,128)S(1)} %get-tuple-element.54) | data formatting | bytes 131072
  35.7 0.6 %copy.26 = f32[64,256]{1,0:T(8,128)} copy(f32[64,256]{1,0:T(8,128)S(1)} %get-tuple-element.57) | data formatting | bytes 131072
  36.3 0.6 %copy.27 = f32[64,256]{1,0:T(8,128)} copy(f32[64,256]{1,0:T(8,128)S(1)} %get-tuple-element.58) | data formatting | bytes 131072
  36.9 0.7 %copy.24 = f32[192,256]{1,0:T(8,128)} copy(f32[192,256]{1,0:T(8,128)S(1)} %get-tuple-element.55) | data formatting | bytes 393216
  37.6 0.7 %copy.25 = f32[192,256]{1,0:T(8,128)} copy(f32[192,256]{1,0:T(8,128)S(1)} %get-tuple-element.56) | data formatting | bytes 393216
  38.3 0.3 project.4
  38.5 0.0 collective-permute-done.10
  38.6 2.7 %collective-permute-done.11 = bf16[24,1792]{1,0:T(8,128)(2,1)S(1)} collective-permute-done((bf16[24,1792]{1,0:T(8,128)(2,1)S(1)}, bf16[24,1792]{1,0:T(8,128)(2,1)S(1)}, u32[]{:S(2)}, u32[]{:S(2)}) %collective-permute-start.11) | collective-permute-done | bytes 86048 | tf_op jit(solution)/shard_map/ppermute | solution.py:42
  41.3 0.0 collective-permute-done.12
  41.3 0.7 %fusion = bf16[1792,24]{0,1:T(8,128)(2,1)} fusion(bf16[24,1792]{1,0:T(8,128)(2,1)S(1)} %collective-permute-done.12, bf16[24,1792]{1,0:T(8,128)(2,1)S(1)} %collective-permute-done.11, f32[24,1792]{1,0:T(8,128)S(1)} %project.4, bf16[24,1792]{1,0:T(8,128)(2,1)S(1)} %collective-permute-done.10), kind=kLoop, calls=%fused_computation.1 | loop fusion | flops 301056 | bytes 516096 | tf_op jit(solution)/shard_map/transpose | solution.py:469
  (8 shorter events, 0.0 us)
Async XLA Ops:
  0.6 15.3 %copy-start.11 = (f32[64,256]{1,0:T(8,128)S(1)}, f32[64,256]{1,0:T(8,128)}, u32[]{:S(2)}) copy-start(f32[64,256]{1,0:T(8,128)} %refs_10_.1) | copy-start | bytes 196612
  0.6 15.3 %copy-start.10 = (f32[64,256]{1,0:T(8,128)S(1)}, f32[64,256]{1,0:T(8,128)}, u32[]{:S(2)}) copy-start(f32[64,256]{1,0:T(8,128)} %refs_9_.1) | copy-start | bytes 196612
  0.7 15.3 %copy-start.8 = (f32[192,256]{1,0:T(8,128)S(1)}, f32[192,256]{1,0:T(8,128)}, u32[]{:S(2)}) copy-start(f32[192,256]{1,0:T(8,128)} %refs_7_.1) | copy-start | bytes 589828
  0.7 15.3 %copy-start.7 = (f32[192,256]{1,0:T(8,128)S(1)}, f32[192,256]{1,0:T(8,128)}, u32[]{:S(2)}) copy-start(f32[192,256]{1,0:T(8,128)} %refs_6_.1) | copy-start | bytes 589828
  0.7 15.3 %copy-start.9 = (f32[64,256]{1,0:T(8,128)S(1)}, f32[64,256]{1,0:T(8,128)}, u32[]{:S(2)}) copy-start(f32[64,256]{1,0:T(8,128)} %refs_8_.1) | copy-start | bytes 196612
  0.7 15.3 %copy-start.6 = (f32[192,256]{1,0:T(8,128)S(1)}, f32[192,256]{1,0:T(8,128)}, u32[]{:S(2)}) copy-start(f32[192,256]{1,0:T(8,128)} %refs_5_.1) | copy-start | bytes 589828
  0.7 3.2 %collective-permute-start = (bf16[1536,256]{1,0:T(8,128)(2,1)}, bf16[1536,256]{1,0:T(8,128)(2,1)S(1)}, u32[]{:S(2)}, u32[]{:S(2)}) collective-permute-start(bf16[1536,256]{1,0:T(8,128)(2,1)} %query_own.1), channel_id=1, source_target_pairs={{0,1},{1,0},{2,3},{3,2},{16,17},{17,16},{18,19},{19,18},{4,5},{5,4... | collective-permute-start | bytes 2359304 | tf_op jit(solution)/shard_map/ppermute | solution.py:42
  1.3 2.7 %collective-permute-start.1 = (bf16[512,256]{1,0:T(8,128)(2,1)}, bf16[512,256]{1,0:T(8,128)(2,1)S(1)}, u32[]{:S(2)}, u32[]{:S(2)}) collective-permute-start(bf16[512,256]{1,0:T(8,128)(2,1)} %key_own.1), channel_id=1, source_target_pairs={{0,1},{1,0},{2,3},{3,2},{16,17},{17,16},{18,19},{19,18},{4,5},{5,4... | collective-permute-start | bytes 786440 | tf_op jit(solution)/shard_map/ppermute | solution.py:42
  2.5 1.4 %collective-permute-start.2 = (bf16[4,24,256]{2,1,0:T(8,128)(2,1)S(1)}, bf16[4,24,256]{2,1,0:T(8,128)(2,1)S(1)}, u32[]{:S(2)}, u32[]{:S(2)}) collective-permute-start(bf16[4,24,256]{2,1,0:T(8,128)(2,1)S(1)} %get-tuple-element.32), channel_id=1, source_target_pairs={{0,1},{1,0},{2,3},{3,2},{16,17},{17,16},{18,19},{19,18},{4,5},{5,4... | collective-permute-start | bytes 147464 | tf_op jit(solution)/shard_map/ppermute | solution.py:42
  3.9 22.3 %slice-start = ((s8[4718592]{0:T(1024)(128)(4,1)}), s8[4194304]{0:T(1024)(128)(4,1)S(1)}, s32[]{:S(2)}) async-start(s8[4718592]{0:T(1024)(128)(4,1)} %bitcast.10), calls=%async_computation | async-start | bytes 8388608
  4.1 7.3 %collective-permute-start.3 = (bf16[304,256]{1,0:T(8,128)(2,1)S(1)}, bf16[304,256]{1,0:T(8,128)(2,1)S(1)}, u32[]{:S(2)}, u32[]{:S(2)}) collective-permute-start(bf16[304,256]{1,0:T(8,128)(2,1)S(1)} %get-tuple-element.35), channel_id=1, source_target_pairs={{0,2},{1,3},{2,0},{3,1},{16,18},{17,19},{18,16},{19,17},{4,6},{5,7... | collective-permute-start | bytes 466952 | tf_op jit(solution)/shard_map/ppermute | solution.py:42
  7.0 6.9 %collective-permute-start.4 = (bf16[304,256]{1,0:T(8,128)(2,1)S(1)}, bf16[304,256]{1,0:T(8,128)(2,1)S(1)}, u32[]{:S(2)}, u32[]{:S(2)}) collective-permute-start(bf16[304,256]{1,0:T(8,128)(2,1)S(1)} %get-tuple-element.36), channel_id=1, source_target_pairs={{0,16},{1,17},{2,18},{3,19},{16,0},{17,1},{18,2},{19,3},{4,20},{5,... | collective-permute-start | bytes 466952 | tf_op jit(solution)/shard_map/ppermute | solution.py:42
  8.5 7.4 %collective-permute-start.5 = (bf16[304,256]{1,0:T(8,128)(2,1)S(1)}, bf16[304,256]{1,0:T(8,128)(2,1)S(1)}, u32[]{:S(2)}, u32[]{:S(2)}) collective-permute-start(bf16[304,256]{1,0:T(8,128)(2,1)S(1)} %get-tuple-element.37), channel_id=1, source_target_pairs={{0,18},{1,19},{2,16},{3,17},{16,2},{17,3},{18,0},{19,1},{4,22},{5,... | collective-permute-start | bytes 466952 | tf_op jit(solution)/shard_map/ppermute | solution.py:42
  16.0 8.9 %copy-start.1 = (bf16[1536,128]{1,0:T(8,128)(2,1)S(1)}, bf16[1536,128]{1,0:T(8,128)(2,1)}, u32[]{:S(2)}) copy-start(bf16[1536,128]{1,0:T(8,128)(2,1)} %weight.5) | copy-start | bytes 1179652
  16.0 8.9 %copy-start.3 = (bf16[8,3,1536]{2,0,1:T(8,128)(2,1)S(1)}, bf16[8,3,1536]{2,0,1:T(8,128)(2,1)}, u32[]{:S(2)}) copy-start(bf16[8,3,1536]{2,0,1:T(8,128)(2,1)} %param.15) | copy-start | bytes 221188
  16.0 8.9 %copy-start.4 = (bf16[8,3,576]{2,0,1:T(8,128)(2,1)S(1)}, bf16[8,3,576]{2,0,1:T(8,128)(2,1)}, u32[]{:S(2)}) copy-start(bf16[8,3,576]{2,0,1:T(8,128)(2,1)} %param.16) | copy-start | bytes 82948
  16.0 8.9 %copy-start.5 = (s32[8]{0:T(128)S(1)}, s32[8]{0:T(128)}, u32[]{:S(2)}) copy-start(s32[8]{0:T(128)} %param.18) | copy-start | bytes 100
  16.0 10.2 %slice-start.1 = ((s8[4718592]{0:T(1024)(128)(4,1)}), s8[524288]{0:T(1024)(128)(4,1)S(1)}, s32[]{:S(2)}) async-start(s8[4718592]{0:T(1024)(128)(4,1)} %bitcast.10), calls=%async_computation.1 | async-start | bytes 1048576
  16.0 10.2 %copy-start.2 = (bf16[512,256]{1,0:T(8,128)(2,1)S(1)}, bf16[512,256]{1,0:T(8,128)(2,1)}, u32[]{:S(2)}) copy-start(bf16[512,256]{1,0:T(8,128)(2,1)} %value_up.1) | copy-start | bytes 786436
  16.4 12.7 %copy-start = (bf16[256,7168]{1,0:T(8,128)(2,1)S(1)}, bf16[256,7168]{1,0:T(8,128)(2,1)}, u32[]{:S(2)}) copy-start(bf16[256,7168]{1,0:T(8,128)(2,1)} %weight.9) | copy-start | bytes 11010052
  16.4 4.2 %collective-permute-start.6 = (bf16[112,256]{1,0:T(8,128)(2,1)S(1)}, bf16[112,256]{1,0:T(8,128)(2,1)S(1)}, u32[]{:S(2)}, u32[]{:S(2)}) collective-permute-start(bf16[112,256]{1,0:T(8,128)(2,1)S(1)} %get-tuple-element.46), channel_id=1, source_target_pairs={{0,2},{1,3},{2,0},{3,1},{16,18},{17,19},{18,16},{19,17},{4,6},{5,7... | collective-permute-start | bytes 172040 | tf_op jit(solution)/shard_map/ppermute | solution.py:42
  18.2 4.2 %collective-permute-start.7 = (bf16[112,256]{1,0:T(8,128)(2,1)S(1)}, bf16[112,256]{1,0:T(8,128)(2,1)S(1)}, u32[]{:S(2)}, u32[]{:S(2)}) collective-permute-start(bf16[112,256]{1,0:T(8,128)(2,1)S(1)} %get-tuple-element.47), channel_id=1, source_target_pairs={{0,16},{1,17},{2,18},{3,19},{16,0},{17,1},{18,2},{19,3},{4,20},{5,... | collective-permute-start | bytes 172040 | tf_op jit(solution)/shard_map/ppermute | solution.py:42
  19.6 5.1 %collective-permute-start.8 = (bf16[112,256]{1,0:T(8,128)(2,1)S(1)}, bf16[112,256]{1,0:T(8,128)(2,1)S(1)}, u32[]{:S(2)}, u32[]{:S(2)}) collective-permute-start(bf16[112,256]{1,0:T(8,128)(2,1)S(1)} %get-tuple-element.48), channel_id=1, source_target_pairs={{0,18},{1,19},{2,16},{3,17},{16,2},{17,3},{18,0},{19,1},{4,22},{5,... | collective-permute-start | bytes 172040 | tf_op jit(solution)/shard_map/ppermute | solution.py:42
  24.8 1.4 %collective-permute-start.9 = (bf16[280,256]{1,0:T(8,128)(2,1)S(1)}, bf16[280,256]{1,0:T(8,128)(2,1)S(1)}, u32[]{:S(2)}, u32[]{:S(2)}) collective-permute-start(bf16[280,256]{1,0:T(8,128)(2,1)S(1)} %get-tuple-element.50.pair_own), channel_id=1, source_target_pairs={{0,1},{1,0},{2,3},{3,2},{16,17},{17,16},{18,19},{19,18},{4,5},{5,4... | collective-permute-start | bytes 430088 | tf_op jit(solution)/shard_map/ppermute | solution.py:42
  29.9 8.6 %collective-permute-start.10 = (bf16[24,1792]{1,0:T(8,128)(2,1)S(1)}, bf16[24,1792]{1,0:T(8,128)(2,1)S(1)}, u32[]{:S(2)}, u32[]{:S(2)}) collective-permute-start(bf16[24,1792]{1,0:T(8,128)(2,1)S(1)} %project.5), channel_id=1, source_target_pairs={{0,4},{4,0},{8,12},{12,8},{1,5},{5,1},{9,13},{13,9},{2,6},{6,2},{1... | collective-permute-start | bytes 258056 | tf_op jit(solution)/shard_map/ppermute | solution.py:42
  31.5 9.8 %collective-permute-start.11 = (bf16[24,1792]{1,0:T(8,128)(2,1)S(1)}, bf16[24,1792]{1,0:T(8,128)(2,1)S(1)}, u32[]{:S(2)}, u32[]{:S(2)}) collective-permute-start(bf16[24,1792]{1,0:T(8,128)(2,1)S(1)} %project.6), channel_id=1, source_target_pairs={{0,8},{4,12},{8,0},{12,4},{1,9},{5,13},{9,1},{13,5},{2,10},{6,14},... | collective-permute-start | bytes 258056 | tf_op jit(solution)/shard_map/ppermute | solution.py:42
  34.1 7.2 %collective-permute-start.12 = (bf16[24,1792]{1,0:T(8,128)(2,1)S(1)}, bf16[24,1792]{1,0:T(8,128)(2,1)S(1)}, u32[]{:S(2)}, u32[]{:S(2)}) collective-permute-start(bf16[24,1792]{1,0:T(8,128)(2,1)S(1)} %project.7), channel_id=1, source_target_pairs={{0,12},{4,8},{8,4},{12,0},{1,13},{5,9},{9,5},{13,1},{2,14},{6,10},... | collective-permute-start | bytes 258056 | tf_op jit(solution)/shard_map/ppermute | solution.py:42

commit v2 on v1

--- a/solution.py
+++ b/solution.py
@@ -63,7 +63,18 @@
     return pl.ds(pl.multiple_of(index * count, 16), count)
 
 
-def own_kernel(query_own, key_own, latents_in, out, keep, give, latents, sems):
+def cut(latents, out, core, chips, count):
+    values = latents[...].astype(jnp.float32)
+    pad = jnp.zeros((values.shape[0], out.shape[2] - count), jnp.float32)
+    for other in range(chips):
+        even, odd = (
+            values[:, (2 * other + i) * count:(2 * other + i + 1) * count] for i in range(2)
+        )
+        chosen = jnp.concatenate([jnp.where(core == 0, even, odd), pad], 1)
+        out[other] = chosen.astype(out.dtype)
+
+
+def own_kernel(query_own, key_own, latents_in, out, keep, latents, sems):
     _, core, chips = place()
     fetch = pltpu.make_async_copy(latents_in, latents, sems.at[2 * chips])
     fetch.start()
@@ -82,19 +93,8 @@
             start += count
     for copy in copies:
         copy.start()
-    count = query_own.shape[0] // (2 * chips)
     fetch.wait()
-    values = latents[...].astype(jnp.float32)
-    pad = jnp.zeros((values.shape[0], keep.shape[2] - count), jnp.float32)
-    for other in range(chips):
-        even, odd = (
-            jnp.concatenate(
-                [values[:, (2 * other + i) * count:(2 * other + i + 1) * count], pad], 1
-            )
-            for i in range(2)
-        )
-        keep[other] = jnp.where(core == 0, even, odd).astype(keep.dtype)
-        give[other] = jnp.where(core == 0, odd, even).astype(give.dtype)
+    cut(latents, keep, core, chips, query_own.shape[0] // (2 * chips))
     for copy in copies:
         copy.wait()
 
@@ -105,10 +105,12 @@
     grad_rows = (query_own.shape[0] + key_own.shape[0]) // (2 * chips)
     return pl.pallas_call(
         own_kernel,
-        out_shape=[jax.ShapeDtypeStruct((chips, grad_rows, width), query_own.dtype)]
-        + [jax.ShapeDtypeStruct((chips, latents.shape[0], width), latents.dtype)] * 2,
+        out_shape=[
+            jax.ShapeDtypeStruct((chips, grad_rows, width), query_own.dtype),
+            jax.ShapeDtypeStruct((chips, latents.shape[0], width), latents.dtype),
+        ],
         in_specs=[HBM_SPEC] * 3,
-        out_specs=[VMEM_SPEC] * 3,
+        out_specs=[VMEM_SPEC] * 2,
         scratch_shapes=[
             pltpu.VMEM(latents.shape, latents.dtype),
             pltpu.SemaphoreType.DMA((2 * chips + 1,)),
@@ -119,10 +121,12 @@
     )(in_hbm(query_own), in_hbm(key_own), in_hbm(latents))
 
 
-def pack_kernel(own, query_got, key_got, latent_own, latent_got, *outs):
+def pack_kernel(own, query_got, key_got, latent_own, latents, *outs):
     chip, core, chips = place()
+    *outs, latent_got = outs
     total, latent_out, packs = outs[0], outs[1], outs[2:]
     grad_rows = total.shape[0]
+    cut(latents, latent_got, core, chips, query_got.shape[0] // (2 * chips))
     for j in range(chips):
         other = chip ^ j
         start = 0
@@ -135,19 +139,19 @@
             else:
                 packs[j - 1][start:start + count, :] = both.astype(jnp.bfloat16)
             start += count
-        latents = jnp.concatenate(
+        pair = jnp.concatenate(
             [latent_own[other].astype(jnp.float32), latent_got[other].astype(jnp.float32)]
         ).astype(jnp.bfloat16)
         if j == 0:
-            latent_out[...] = latents
+            latent_out[...] = pair
         else:
-            packs[j - 1][grad_rows:, :] = latents
-
-
-def pack_sums(own, query_got, key_got, latent_own, latent_got):
+            packs[j - 1][grad_rows:, :] = pair
+
+
+def pack_sums(own, query_got, key_got, latent_own, latents):
     chips, grad_rows, width = own.shape
     tokens = latent_own.shape[1]
-    total, latents, *packs = pl.pallas_call(
+    total, columns, *packs = pl.pallas_call(
         pack_kernel,
         out_shape=[
             jax.ShapeDtypeStruct((grad_rows, width), jnp.float32),
@@ -156,11 +160,12 @@
         + [jax.ShapeDtypeStruct((grad_rows + 2 * tokens, width), jnp.bfloat16)] * (chips - 1),
         in_specs=[VMEM_SPEC] * 5,
         out_specs=[VMEM_SPEC] * (chips + 1),
+        scratch_shapes=[pltpu.VMEM(latent_own.shape, latent_own.dtype)],
         compiler_params=pltpu.CompilerParams(vmem_limit_bytes=8 << 20),
         cost_estimate=pl.CostEstimate(flops=10**9, bytes_accessed=10**6, transcendentals=0),
         name="pack",
-    )(own, query_got, key_got, latent_own, latent_got)
-    return total, latents, packs
+    )(own, query_got, key_got, latent_own, latents)
+    return total, columns, packs
 
 
 def row_value(lengths, count, rows):
@@ -169,7 +174,9 @@
     return jnp.sum(jnp.where(token % rows == row, lengths, 0), 1, keepdims=True)
 
 
-def rope_kernel(after, query, weight, entries, lengths, query_rope, new_keys):
+def rope_kernel(
+    after, query, weight, entries, lengths, cache, query_rope, new_keys, scores_out
+):
     del after
     tokens, rows = query.shape[0], lengths.shape[1]
     half = R // 2
@@ -187,26 +194,34 @@
 
     projected = jnp.dot(query[...], weight[...], preferred_element_type=jnp.float32)
     heads = projected.shape[1] // R
-    query_rope[...] = jnp.concatenate(
+    turned = jnp.concatenate(
         [turn(projected[:, h * R:(h + 1) * R]) for h in range(heads)]
     ).astype(jnp.bfloat16)
+    query_rope[...] = turned
+    batch_of = lax.broadcasted_iota(jnp.int32, (heads * tokens, 1), 0) % rows
+    scores = jnp.zeros(scores_out.shape, jnp.float32)
+    for b in range(rows):
+        here = jnp.dot(turned, cache[b, KL:, :], preferred_element_type=jnp.float32)
+        scores = jnp.where(batch_of == b, here, scores)
+    scores_out[...] = scores
     new_keys[:, :KL] = entries[:, :KL]
     new_keys[:, KL:] = turn(entries[:, KL:].astype(jnp.float32)).astype(jnp.bfloat16)
 
 
-def rope(after, query, weight, entries, lengths):
+def rope(after, query, weight, entries, lengths, cache):
     heads = weight.shape[1] // R
     return pl.pallas_call(
         rope_kernel,
         out_shape=[
             jax.ShapeDtypeStruct((heads * query.shape[0], R), jnp.bfloat16),
             jax.ShapeDtypeStruct(entries.shape, jnp.bfloat16),
+            jax.ShapeDtypeStruct((heads * query.shape[0], CACHE), jnp.float32),
         ],
-        in_specs=[VMEM_SPEC] * 5,
-        out_specs=[VMEM_SPEC] * 2,
+        in_specs=[VMEM_SPEC] * 6,
+        out_specs=[VMEM_SPEC] * 3,
         compiler_params=pltpu.CompilerParams(vmem_limit_bytes=4 << 20),
         name="rope",
-    )(after, query, weight, entries, lengths)
+    )(after, query, weight, entries, lengths, cache)
 
 
 def update_kernel(chips, *refs):
@@ -296,7 +311,7 @@
 
 def attend_kernel(
     rows,
-    query_sum, pair_own, pair_got, query_rope, new_keys, lengths, value_up, cache,
+    query_sum, pair_own, pair_got, query_rope, new_keys, rope_scores, lengths, value_up, cache,
     out, key_full,
 ):
     f32, bf16 = jnp.float32, jnp.bfloat16
@@ -328,10 +343,10 @@
     batch_of, step_of = row_of % rows, (row_of // rows) % STEPS
     scores = jnp.zeros((count, CACHE), f32)
     for b in range(rows):
-        here = dot(latent_query, cache[b, :KL, :], nn) + dot(rope, cache[b, KL:, :], nn)
+        here = dot(latent_query, cache[b, :KL, :], nn)
         scores = jnp.where(batch_of == b, here, scores)
     slot = lax.broadcasted_iota(jnp.int32, (count, CACHE), 1)
-    scores = jnp.where(slot < row_value(lengths[...], count, rows), scores * scale, -jnp.inf)
+    scores = jnp.where(slot < row_value(lengths[...], count, rows), (scores + rope_scores[...]) * scale, -jnp.inf)
     fresh = dot(latent_query, new_keys[:, :KL], nt) + dot(rope, new_keys[:, KL:], nt)
     key_at = lax.broadcasted_iota(jnp.int32, (count, tokens), 1)
     seen = (key_at % rows == batch_of) & (key_at // rows <= step_of)
@@ -361,17 +376,22 @@
     out[...] = dot(order, head_values, nn).astype(bf16)
 
 
-def attend(query_sum, pair_own, pair_got, query_rope, new_keys, lengths, value_up, cache):
+def attend(
+    query_sum, pair_own, pair_got, query_rope, new_keys, rope_scores, lengths, value_up, cache
+):
     tokens, width = query_sum.shape
     return pl.pallas_call(
         functools.partial(attend_kernel, lengths.shape[0]),
         out_shape=jax.ShapeDtypeStruct((tokens, width), jnp.bfloat16),
-        in_specs=[VMEM_SPEC] * 8,
+        in_specs=[VMEM_SPEC] * 9,
         out_specs=VMEM_SPEC,
         scratch_shapes=[pltpu.VMEM((KL, width), jnp.bfloat16)],
         compiler_params=pltpu.CompilerParams(vmem_limit_bytes=16 << 20),
         name="attend",
-    )(query_sum, pair_own, pair_got, query_rope, new_keys, lengths[None, :], value_up, cache)
+    )(
+        query_sum, pair_own, pair_got, query_rope, new_keys, rope_scores, lengths[None, :],
+        value_up, cache,
+    )
 
 
 def project_kernel(distance, head_values, weight, out):
@@ -439,15 +459,17 @@
 
     query_got = swap(query_grads, ROW_AXES, devices, 1)
     key_got = swap(key_grads, ROW_AXES, devices, 1)
-    own, latent_keep, latent_give = own_blocks(query_grads, key_grads, flat_query)
-    latent_got = swap(latent_give, ROW_AXES, devices, 1)
-    total, columns, packs = pack_sums(own, query_got, key_got, latent_keep, latent_got)
-    query_rope, new_keys = rope(
+    latent_got = swap(flat_query, ROW_AXES, devices, 1)
+    own, latent_own = own_blocks(query_grads, key_grads, flat_query)
+    total, columns, packs = pack_sums(own, query_got, key_got, latent_own, latent_got)
+    cache = latent_cache.transpose(0, 2, 1)
+    query_rope, new_keys, rope_scores = rope(
         columns,
         flat_query,
         rope_query,
         new_entries.transpose(1, 0, 2).reshape(tokens, KL + R),
         lengths[None, :],
+        cache,
     )
     packs = [swap(pack, ROW_AXES, devices, 2 * j + 2) for j, pack in enumerate(packs)]
 
@@ -458,8 +480,8 @@
     query_sum, pair_own = merge(query_sum, key_half, gots)
     pair_got = swap(pair_own, ROW_AXES, devices, 1)
     head_values = attend(
-        query_sum, pair_own, pair_got, query_rope, new_keys, lengths, value_up,
-        latent_cache.transpose(0, 2, 1),
+        query_sum, pair_own, pair_got, query_rope, new_keys, rope_scores, lengths, value_up,
+        cache,
     )
     attended, *give = project_all(head_values, output_weight)
     shares = lax.axis_size("fsdp")

time: 42.1 us -> 42 us (level)
  transfers between devices with their start and end apart: 13 -> 13, of which waited for: 9 -> 9; matrix products, arithmetic and copies ran while one was open for 9% -> 9% of each run, Pallas kernels for 4% -> 5%
where the time goes in v2:
time: 42 us; the launch traced here: 41.9 us
  waiting for transfers between devices  16.4 us (39%)
  starting transfers between devices  13.6 us (32%)
  Pallas kernels  6.31 us (15%)
  local copies, waits for them, and re-layouts  3.99 us (10%)
  between operations  0.87 us (2%)
  other arithmetic  0.69 us (2%)
    ppermute x13, waiting for transfers between devices, swap(): return lax.ppermute(value, axes, [(i, i ^ distance) for i in range(count)])  16.4 us
    ppermute x13, starting transfers between devices, swap(): return lax.ppermute(value, axes, [(i, i ^ distance) for i in range(count)])  13.6 us
    unnamed x34, local copies, waits for them, and re-layouts  3.99 us
    pallas_call x1, Pallas kernels, attend(): pl.pallas_call(functools.partial(attend_kernel, lengths.shape[0]), out_sh...  2.78 us
    pallas_call x1, Pallas kernels, own_blocks(): pl.pallas_call(own_kernel, out_shape=[jax.ShapeDtypeStruct((chips, grad_r...  1.2 us
    pallas_call x4, Pallas kernels, project(): pl.pallas_call(functools.partial(project_kernel, distance), out_shape=jax...  1.14 us
  transfers between devices with their start and end apart: 13, of which 9 were waited for; matrix products, arithmetic and copies ran while one was open for 9% of the time, Pallas kernels for 5%

profile of v2, /device:TPU:0, one launch (start us, length us, event | category | flops | bytes accessed | tf_op | source)
XLA Modules:
  0.0 41.9 jit_solution(660349048192369790)
XLA Ops:
  0.6 0.0 copy-start.11
  0.6 0.0 copy-start.10
  0.7 0.0 copy-start.8
  0.7 0.0 copy-start.7
  0.7 0.0 copy-start.9
  0.7 0.0 copy-start.6
  0.7 0.6 %collective-permute-start = (bf16[1536,256]{1,0:T(8,128)(2,1)}, bf16[1536,256]{1,0:T(8,128)(2,1)S(1)}, u32[]{:S(2)}, u32[]{:S(2)}) collective-permute-start(bf16[1536,256]{1,0:T(8,128)(2,1)} %query_own.1), channel_id=1, source_target_pairs={{0,1},{1,0},{2,3},{3,2},{16,17},{17,16},{18,19},{19,18},{4,5},{5,4... | collective-permute-start | bytes 2359304 | tf_op jit(solution)/shard_map/ppermute | solution.py:42
  1.3 0.1 collective-permute-start.1
  1.3 0.4 %collective-permute-start.2 = (bf16[24,1536]{1,0:T(8,128)(2,1)}, bf16[24,1536]{1,0:T(8,128)(2,1)S(1)}, u32[]{:S(2)}, u32[]{:S(2)}) collective-permute-start(bf16[24,1536]{1,0:T(8,128)(2,1)} %bitcast.14), channel_id=1, source_target_pairs={{0,1},{1,0},{2,3},{3,2},{16,17},{17,16},{18,19},{19,18},{4,5},{5,4... | collective-permute-start | bytes 221192 | tf_op jit(solution)/shard_map/ppermute | solution.py:42
  1.8 1.2 %own.1 = (bf16[4,256,256]{2,1,0:T(8,128)(2,1)S(1)}, bf16[4,24,256]{2,1,0:T(8,128)(2,1)S(1)}) custom-call(bf16[1536,256]{1,0:T(8,128)(2,1)} %query_own.1, bf16[512,256]{1,0:T(8,128)(2,1)} %key_own.1, bf16[24,1536]{1,0:T(8,128)(2,1)} %bitcast.15), custom_call_target="tpu_custom_call" | custom-call | flops 1000000000 | bytes 1000000 | tf_op jit(solution)/shard_map/own/pallas_call | solution.py:106
  3.0 0.9 %collective-permute-done.2.latents = bf16[24,1536]{1,0:T(8,128)(2,1)S(1)} collective-permute-done((bf16[24,1536]{1,0:T(8,128)(2,1)}, bf16[24,1536]{1,0:T(8,128)(2,1)S(1)}, u32[]{:S(2)}, u32[]{:S(2)}) %collective-permute-start.2) | collective-permute-done | bytes 73760 | tf_op jit(solution)/shard_map/ppermute | solution.py:42
  3.9 0.0 collective-permute-done.1.key_got
  3.9 0.0 collective-permute-done.query_got
  3.9 0.2 pack.1
  4.0 2.9 %collective-permute-start.3 = (bf16[304,256]{1,0:T(8,128)(2,1)S(1)}, bf16[304,256]{1,0:T(8,128)(2,1)S(1)}, u32[]{:S(2)}, u32[]{:S(2)}) collective-permute-start(bf16[304,256]{1,0:T(8,128)(2,1)S(1)} %get-tuple-element.34), channel_id=1, source_target_pairs={{0,2},{1,3},{2,0},{3,1},{16,18},{17,19},{18,16},{19,17},{4,6},{5,7... | collective-permute-start | bytes 466952 | tf_op jit(solution)/shard_map/ppermute | solution.py:42
  7.0 1.5 %collective-permute-start.4 = (bf16[304,256]{1,0:T(8,128)(2,1)S(1)}, bf16[304,256]{1,0:T(8,128)(2,1)S(1)}, u32[]{:S(2)}, u32[]{:S(2)}) collective-permute-start(bf16[304,256]{1,0:T(8,128)(2,1)S(1)} %get-tuple-element.35), channel_id=1, source_target_pairs={{0,16},{1,17},{2,18},{3,19},{16,0},{17,1},{18,2},{19,3},{4,20},{5,... | collective-permute-start | bytes 466952 | tf_op jit(solution)/shard_map/ppermute | solution.py:42
  8.5 0.1 collective-permute-start.5
  8.5 2.8 %collective-permute-done.3.refs_2_ = bf16[304,256]{1,0:T(8,128)(2,1)S(1)} collective-permute-done((bf16[304,256]{1,0:T(8,128)(2,1)S(1)}, bf16[304,256]{1,0:T(8,128)(2,1)S(1)}, u32[]{:S(2)}, u32[]{:S(2)}) %collective-permute-start.3) | collective-permute-done | bytes 155680 | tf_op jit(solution)/shard_map/ppermute | solution.py:42
  11.3 2.6 %collective-permute-done.4.refs_3_ = bf16[304,256]{1,0:T(8,128)(2,1)S(1)} collective-permute-done((bf16[304,256]{1,0:T(8,128)(2,1)S(1)}, bf16[304,256]{1,0:T(8,128)(2,1)S(1)}, u32[]{:S(2)}, u32[]{:S(2)}) %collective-permute-start.4) | collective-permute-done | bytes 155680 | tf_op jit(solution)/shard_map/ppermute | solution.py:42
  13.9 2.0 %collective-permute-done.5.refs_4_ = bf16[304,256]{1,0:T(8,128)(2,1)S(1)} collective-permute-done((bf16[304,256]{1,0:T(8,128)(2,1)S(1)}, bf16[304,256]{1,0:T(8,128)(2,1)S(1)}, u32[]{:S(2)}, u32[]{:S(2)}) %collective-permute-start.5) | collective-permute-done | bytes 155680 | tf_op jit(solution)/shard_map/ppermute | solution.py:42
  15.9 0.0 copy-done.11
  15.9 0.0 copy-done.10
  15.9 0.0 copy-done.8
  15.9 0.0 copy-done.7
  15.9 0.0 copy-done.9
  15.9 0.0 copy-done.6
  15.9 0.0 slice-start.1
  16.0 0.0 copy-start.1
  16.0 0.0 copy-start.3
  16.0 0.0 copy-start.4
  16.0 0.0 copy-start.5
  16.0 0.4 update.1
  16.4 0.0 copy-start.2
  16.4 1.7 %collective-permute-start.6 = (bf16[112,256]{1,0:T(8,128)(2,1)S(1)}, bf16[112,256]{1,0:T(8,128)(2,1)S(1)}, u32[]{:S(2)}, u32[]{:S(2)}) collective-permute-start(bf16[112,256]{1,0:T(8,128)(2,1)S(1)} %get-tuple-element.45), channel_id=1, source_target_pairs={{0,2},{1,3},{2,0},{3,1},{16,18},{17,19},{18,16},{19,17},{4,6},{5,7... | collective-permute-start | bytes 172040 | tf_op jit(solution)/shard_map/ppermute | solution.py:42
  18.1 1.5 %collective-permute-start.7 = (bf16[112,256]{1,0:T(8,128)(2,1)S(1)}, bf16[112,256]{1,0:T(8,128)(2,1)S(1)}, u32[]{:S(2)}, u32[]{:S(2)}) collective-permute-start(bf16[112,256]{1,0:T(8,128)(2,1)S(1)} %get-tuple-element.46), channel_id=1, source_target_pairs={{0,16},{1,17},{2,18},{3,19},{16,0},{17,1},{18,2},{19,3},{4,20},{5,... | collective-permute-start | bytes 172040 | tf_op jit(solution)/shard_map/ppermute | solution.py:42
  19.6 0.3 collective-permute-start.8
  20.0 0.7 %collective-permute-done.6.refs_0_ = bf16[112,256]{1,0:T(8,128)(2,1)S(1)} collective-permute-done((bf16[112,256]{1,0:T(8,128)(2,1)S(1)}, bf16[112,256]{1,0:T(8,128)(2,1)S(1)}, u32[]{:S(2)}, u32[]{:S(2)}) %collective-permute-start.6) | collective-permute-done | bytes 57376 | tf_op jit(solution)/shard_map/ppermute | solution.py:42
  20.6 1.7 %collective-permute-done.7.refs_1_ = bf16[112,256]{1,0:T(8,128)(2,1)S(1)} collective-permute-done((bf16[112,256]{1,0:T(8,128)(2,1)S(1)}, bf16[112,256]{1,0:T(8,128)(2,1)S(1)}, u32[]{:S(2)}, u32[]{:S(2)}) %collective-permute-start.7) | collective-permute-done | bytes 57376 | tf_op jit(solution)/shard_map/ppermute | solution.py:42
  22.3 2.4 %collective-permute-done.8.refs_2_ = bf16[112,256]{1,0:T(8,128)(2,1)S(1)} collective-permute-done((bf16[112,256]{1,0:T(8,128)(2,1)S(1)}, bf16[112,256]{1,0:T(8,128)(2,1)S(1)}, u32[]{:S(2)}, u32[]{:S(2)}) %collective-permute-start.8) | collective-permute-done | bytes 57376 | tf_op jit(solution)/shard_map/ppermute | solution.py:42
  24.7 0.1 collective-permute-start.9
  24.8 0.0 slice-done
  24.8 0.0 slice-done.1
  24.9 0.0 copy-start
  24.9 0.6 %rope.1 = (bf16[48,64]{1,0:T(8,128)(2,1)S(1)}, bf16[24,576]{1,0:T(8,128)(2,1)S(1)}, f32[48,512]{1,0:T(8,128)S(1)}) custom-call(bf16[48,256]{1,0:T(8,128)(2,1)S(1)} %get-tuple-element.33.refs_1_.after, bf16[24,1536]{1,0:T(8,128)(2,1)S(1)} %bitcast.16, bf16[1536,128]{1,0:T(8,128)(2,1)S(1)} %copy-done.1, bf16[24,576]{1,0:T(8,128)(2,1)S(1)} %bitcast.17, ...), custom_call_target="tpu_custom_call" | custom-call | tf_op jit(solution)/shard_map/rope/pallas_call | solution.py:213
  25.5 0.7 %collective-permute-done.9.pair_got = bf16[280,256]{1,0:T(8,128)(2,1)S(1)} collective-permute-done((bf16[280,256]{1,0:T(8,128)(2,1)S(1)}, bf16[280,256]{1,0:T(8,128)(2,1)S(1)}, u32[]{:S(2)}, u32[]{:S(2)}) %collective-permute-start.9) | collective-permute-done | bytes 143392 | tf_op jit(solution)/shard_map/ppermute | solution.py:42
  26.2 0.0 copy-done.2
  26.2 2.8 %attend.1.head_values = bf16[24,256]{1,0:T(8,128)(2,1)S(1)} custom-call(f32[24,256]{1,0:T(8,128)S(1)} %get-tuple-element.48.query_sum, bf16[280,256]{1,0:T(8,128)(2,1)S(1)} %get-tuple-element.49.pair_own, bf16[280,256]{1,0:T(8,128)(2,1)S(1)} %collective-permute-done.9.pair_got, bf16[48,64]{1,0:T(8,128)(2,1)S(1)} %get-tuple-element.50.query_rope, ...), custom_call_target="tpu_custom_call" | custom-call | tf_op jit(solution)/shard_map/attend/pallas_call | solution.py:383
  29.0 0.3 project.7
  29.2 0.3 project.6
  29.5 0.3 project.5
  29.8 1.6 %collective-permute-start.10 = (bf16[24,1792]{1,0:T(8,128)(2,1)S(1)}, bf16[24,1792]{1,0:T(8,128)(2,1)S(1)}, u32[]{:S(2)}, u32[]{:S(2)}) collective-permute-start(bf16[24,1792]{1,0:T(8,128)(2,1)S(1)} %project.5), channel_id=1, source_target_pairs={{0,4},{4,0},{8,12},{12,8},{1,5},{5,1},{9,13},{13,9},{2,6},{6,2},{1... | collective-permute-start | bytes 258056 | tf_op jit(solution)/shard_map/ppermute | solution.py:42
  31.4 2.6 %collective-permute-start.11 = (bf16[24,1792]{1,0:T(8,128)(2,1)S(1)}, bf16[24,1792]{1,0:T(8,128)(2,1)S(1)}, u32[]{:S(2)}, u32[]{:S(2)}) collective-permute-start(bf16[24,1792]{1,0:T(8,128)(2,1)S(1)} %project.6), channel_id=1, source_target_pairs={{0,8},{4,12},{8,0},{12,4},{1,9},{5,13},{9,1},{13,5},{2,10},{6,14},... | collective-permute-start | bytes 258056 | tf_op jit(solution)/shard_map/ppermute | solution.py:42
  34.0 0.2 collective-permute-start.12
  34.2 0.7 %copy.22 = f32[192,256]{1,0:T(8,128)} copy(f32[192,256]{1,0:T(8,128)S(1)} %get-tuple-element.53) | data formatting | bytes 393216
  34.9 0.6 %copy.23 = f32[64,256]{1,0:T(8,128)} copy(f32[64,256]{1,0:T(8,128)S(1)} %get-tuple-element.54) | data formatting | bytes 131072
  35.5 0.6 %copy.26 = f32[64,256]{1,0:T(8,128)} copy(f32[64,256]{1,0:T(8,128)S(1)} %get-tuple-element.57) | data formatting | bytes 131072
  36.2 0.6 %copy.27 = f32[64,256]{1,0:T(8,128)} copy(f32[64,256]{1,0:T(8,128)S(1)} %get-tuple-element.58) | data formatting | bytes 131072
  36.8 0.7 %copy.24 = f32[192,256]{1,0:T(8,128)} copy(f32[192,256]{1,0:T(8,128)S(1)} %get-tuple-element.55) | data formatting | bytes 393216
  37.5 0.7 %copy.25 = f32[192,256]{1,0:T(8,128)} copy(f32[192,256]{1,0:T(8,128)S(1)} %get-tuple-element.56) | data formatting | bytes 393216
  38.2 0.3 project.4
  38.4 0.0 collective-permute-done.10
  38.4 2.8 %collective-permute-done.11 = bf16[24,1792]{1,0:T(8,128)(2,1)S(1)} collective-permute-done((bf16[24,1792]{1,0:T(8,128)(2,1)S(1)}, bf16[24,1792]{1,0:T(8,128)(2,1)S(1)}, u32[]{:S(2)}, u32[]{:S(2)}) %collective-permute-start.11) | collective-permute-done | bytes 86048 | tf_op jit(solution)/shard_map/ppermute | solution.py:42
  41.2 0.0 collective-permute-done.12
  41.2 0.7 %fusion = bf16[1792,24]{0,1:T(8,128)(2,1)} fusion(bf16[24,1792]{1,0:T(8,128)(2,1)S(1)} %collective-permute-done.12, bf16[24,1792]{1,0:T(8,128)(2,1)S(1)} %collective-permute-done.11, f32[24,1792]{1,0:T(8,128)S(1)} %project.4, bf16[24,1792]{1,0:T(8,128)(2,1)S(1)} %collective-permute-done.10), kind=kLoop, calls=%fused_computation.1 | loop fusion | flops 301056 | bytes 516096 | tf_op jit(solution)/shard_map/transpose | solution.py:491
  (8 shorter events, 0.0 us)
Async XLA Ops:
  0.6 15.3 %copy-start.11 = (f32[64,256]{1,0:T(8,128)S(1)}, f32[64,256]{1,0:T(8,128)}, u32[]{:S(2)}) copy-start(f32[64,256]{1,0:T(8,128)} %refs_10_.1) | copy-start | bytes 196612
  0.6 15.3 %copy-start.10 = (f32[64,256]{1,0:T(8,128)S(1)}, f32[64,256]{1,0:T(8,128)}, u32[]{:S(2)}) copy-start(f32[64,256]{1,0:T(8,128)} %refs_9_.1) | copy-start | bytes 196612
  0.7 15.3 %copy-start.8 = (f32[192,256]{1,0:T(8,128)S(1)}, f32[192,256]{1,0:T(8,128)}, u32[]{:S(2)}) copy-start(f32[192,256]{1,0:T(8,128)} %refs_7_.1) | copy-start | bytes 589828
  0.7 15.3 %copy-start.7 = (f32[192,256]{1,0:T(8,128)S(1)}, f32[192,256]{1,0:T(8,128)}, u32[]{:S(2)}) copy-start(f32[192,256]{1,0:T(8,128)} %refs_6_.1) | copy-start | bytes 589828
  0.7 15.3 %copy-start.9 = (f32[64,256]{1,0:T(8,128)S(1)}, f32[64,256]{1,0:T(8,128)}, u32[]{:S(2)}) copy-start(f32[64,256]{1,0:T(8,128)} %refs_8_.1) | copy-start | bytes 196612
  0.7 15.3 %copy-start.6 = (f32[192,256]{1,0:T(8,128)S(1)}, f32[192,256]{1,0:T(8,128)}, u32[]{:S(2)}) copy-start(f32[192,256]{1,0:T(8,128)} %refs_5_.1) | copy-start | bytes 589828
  0.7 3.2 %collective-permute-start = (bf16[1536,256]{1,0:T(8,128)(2,1)}, bf16[1536,256]{1,0:T(8,128)(2,1)S(1)}, u32[]{:S(2)}, u32[]{:S(2)}) collective-permute-start(bf16[1536,256]{1,0:T(8,128)(2,1)} %query_own.1), channel_id=1, source_target_pairs={{0,1},{1,0},{2,3},{3,2},{16,17},{17,16},{18,19},{19,18},{4,5},{5,4... | collective-permute-start | bytes 2359304 | tf_op jit(solution)/shard_map/ppermute | solution.py:42
  1.3 2.6 %collective-permute-start.1 = (bf16[512,256]{1,0:T(8,128)(2,1)}, bf16[512,256]{1,0:T(8,128)(2,1)S(1)}, u32[]{:S(2)}, u32[]{:S(2)}) collective-permute-start(bf16[512,256]{1,0:T(8,128)(2,1)} %key_own.1), channel_id=1, source_target_pairs={{0,1},{1,0},{2,3},{3,2},{16,17},{17,16},{18,19},{19,18},{4,5},{5,4... | collective-permute-start | bytes 786440 | tf_op jit(solution)/shard_map/ppermute | solution.py:42
  1.3 2.5 %collective-permute-start.2 = (bf16[24,1536]{1,0:T(8,128)(2,1)}, bf16[24,1536]{1,0:T(8,128)(2,1)S(1)}, u32[]{:S(2)}, u32[]{:S(2)}) collective-permute-start(bf16[24,1536]{1,0:T(8,128)(2,1)} %bitcast.14), channel_id=1, source_target_pairs={{0,1},{1,0},{2,3},{3,2},{16,17},{17,16},{18,19},{19,18},{4,5},{5,4... | collective-permute-start | bytes 221192 | tf_op jit(solution)/shard_map/ppermute | solution.py:42
  3.9 20.9 %slice-start = ((s8[4718592]{0:T(1024)(128)(4,1)}), s8[4194304]{0:T(1024)(128)(4,1)S(1)}, s32[]{:S(2)}) async-start(s8[4718592]{0:T(1024)(128)(4,1)} %bitcast.10), calls=%async_computation | async-start | bytes 8388608
  4.0 7.3 %collective-permute-start.3 = (bf16[304,256]{1,0:T(8,128)(2,1)S(1)}, bf16[304,256]{1,0:T(8,128)(2,1)S(1)}, u32[]{:S(2)}, u32[]{:S(2)}) collective-permute-start(bf16[304,256]{1,0:T(8,128)(2,1)S(1)} %get-tuple-element.34), channel_id=1, source_target_pairs={{0,2},{1,3},{2,0},{3,1},{16,18},{17,19},{18,16},{19,17},{4,6},{5,7... | collective-permute-start | bytes 466952 | tf_op jit(solution)/shard_map/ppermute | solution.py:42
  7.0 6.9 %collective-permute-start.4 = (bf16[304,256]{1,0:T(8,128)(2,1)S(1)}, bf16[304,256]{1,0:T(8,128)(2,1)S(1)}, u32[]{:S(2)}, u32[]{:S(2)}) collective-permute-start(bf16[304,256]{1,0:T(8,128)(2,1)S(1)} %get-tuple-element.35), channel_id=1, source_target_pairs={{0,16},{1,17},{2,18},{3,19},{16,0},{17,1},{18,2},{19,3},{4,20},{5,... | collective-permute-start | bytes 466952 | tf_op jit(solution)/shard_map/ppermute | solution.py:42
  8.5 7.4 %collective-permute-start.5 = (bf16[304,256]{1,0:T(8,128)(2,1)S(1)}, bf16[304,256]{1,0:T(8,128)(2,1)S(1)}, u32[]{:S(2)}, u32[]{:S(2)}) collective-permute-start(bf16[304,256]{1,0:T(8,128)(2,1)S(1)} %get-tuple-element.36), channel_id=1, source_target_pairs={{0,18},{1,19},{2,16},{3,17},{16,2},{17,3},{18,0},{19,1},{4,22},{5,... | collective-permute-start | bytes 466952 | tf_op jit(solution)/shard_map/ppermute | solution.py:42
  15.9 8.9 %slice-start.1 = ((s8[4718592]{0:T(1024)(128)(4,1)}), s8[524288]{0:T(1024)(128)(4,1)S(1)}, s32[]{:S(2)}) async-start(s8[4718592]{0:T(1024)(128)(4,1)} %bitcast.10), calls=%async_computation.1 | async-start | bytes 1048576
  16.0 8.9 %copy-start.1 = (bf16[1536,128]{1,0:T(8,128)(2,1)S(1)}, bf16[1536,128]{1,0:T(8,128)(2,1)}, u32[]{:S(2)}) copy-start(bf16[1536,128]{1,0:T(8,128)(2,1)} %weight.5) | copy-start | bytes 1179652
  16.0 8.9 %copy-start.3 = (bf16[8,3,1536]{2,0,1:T(8,128)(2,1)S(1)}, bf16[8,3,1536]{2,0,1:T(8,128)(2,1)}, u32[]{:S(2)}) copy-start(bf16[8,3,1536]{2,0,1:T(8,128)(2,1)} %param.15) | copy-start | bytes 221188
  16.0 8.9 %copy-start.4 = (bf16[8,3,576]{2,0,1:T(8,128)(2,1)S(1)}, bf16[8,3,576]{2,0,1:T(8,128)(2,1)}, u32[]{:S(2)}) copy-start(bf16[8,3,576]{2,0,1:T(8,128)(2,1)} %param.16) | copy-start | bytes 82948
  16.0 8.9 %copy-start.5 = (s32[8]{0:T(128)S(1)}, s32[8]{0:T(128)}, u32[]{:S(2)}) copy-start(s32[8]{0:T(128)} %param.18) | copy-start | bytes 100
  16.4 9.8 %copy-start.2 = (bf16[512,256]{1,0:T(8,128)(2,1)S(1)}, bf16[512,256]{1,0:T(8,128)(2,1)}, u32[]{:S(2)}) copy-start(bf16[512,256]{1,0:T(8,128)(2,1)} %value_up.1) | copy-start | bytes 786436
  16.4 4.2 %collective-permute-start.6 = (bf16[112,256]{1,0:T(8,128)(2,1)S(1)}, bf16[112,256]{1,0:T(8,128)(2,1)S(1)}, u32[]{:S(2)}, u32[]{:S(2)}) collective-permute-start(bf16[112,256]{1,0:T(8,128)(2,1)S(1)} %get-tuple-element.45), channel_id=1, source_target_pairs={{0,2},{1,3},{2,0},{3,1},{16,18},{17,19},{18,16},{19,17},{4,6},{5,7... | collective-permute-start | bytes 172040 | tf_op jit(solution)/shard_map/ppermute | solution.py:42
  18.1 4.2 %collective-permute-start.7 = (bf16[112,256]{1,0:T(8,128)(2,1)S(1)}, bf16[112,256]{1,0:T(8,128)(2,1)S(1)}, u32[]{:S(2)}, u32[]{:S(2)}) collective-permute-start(bf16[112,256]{1,0:T(8,128)(2,1)S(1)} %get-tuple-element.46), channel_id=1, source_target_pairs={{0,16},{1,17},{2,18},{3,19},{16,0},{17,1},{18,2},{19,3},{4,20},{5,... | collective-permute-start | bytes 172040 | tf_op jit(solution)/shard_map/ppermute | solution.py:42
  19.6 5.1 %collective-permute-start.8 = (bf16[112,256]{1,0:T(8,128)(2,1)S(1)}, bf16[112,256]{1,0:T(8,128)(2,1)S(1)}, u32[]{:S(2)}, u32[]{:S(2)}) collective-permute-start(bf16[112,256]{1,0:T(8,128)(2,1)S(1)} %get-tuple-element.47), channel_id=1, source_target_pairs={{0,18},{1,19},{2,16},{3,17},{16,2},{17,3},{18,0},{19,1},{4,22},{5,... | collective-permute-start | bytes 172040 | tf_op jit(solution)/shard_map/ppermute | solution.py:42
  24.7 1.4 %collective-permute-start.9 = (bf16[280,256]{1,0:T(8,128)(2,1)S(1)}, bf16[280,256]{1,0:T(8,128)(2,1)S(1)}, u32[]{:S(2)}, u32[]{:S(2)}) collective-permute-start(bf16[280,256]{1,0:T(8,128)(2,1)S(1)} %get-tuple-element.49.pair_own), channel_id=1, source_target_pairs={{0,1},{1,0},{2,3},{3,2},{16,17},{17,16},{18,19},{19,18},{4,5},{5,4... | collective-permute-start | bytes 430088 | tf_op jit(solution)/shard_map/ppermute | solution.py:42
  24.9 4.1 %copy-start = (bf16[256,7168]{1,0:T(8,128)(2,1)S(1)}, bf16[256,7168]{1,0:T(8,128)(2,1)}, u32[]{:S(2)}) copy-start(bf16[256,7168]{1,0:T(8,128)(2,1)} %weight.9) | copy-start | bytes 11010052
  29.8 8.6 %collective-permute-start.10 = (bf16[24,1792]{1,0:T(8,128)(2,1)S(1)}, bf16[24,1792]{1,0:T(8,128)(2,1)S(1)}, u32[]{:S(2)}, u32[]{:S(2)}) collective-permute-start(bf16[24,1792]{1,0:T(8,128)(2,1)S(1)} %project.5), channel_id=1, source_target_pairs={{0,4},{4,0},{8,12},{12,8},{1,5},{5,1},{9,13},{13,9},{2,6},{6,2},{1... | collective-permute-start | bytes 258056 | tf_op jit(solution)/shard_map/ppermute | solution.py:42
  31.4 9.8 %collective-permute-start.11 = (bf16[24,1792]{1,0:T(8,128)(2,1)S(1)}, bf16[24,1792]{1,0:T(8,128)(2,1)S(1)}, u32[]{:S(2)}, u32[]{:S(2)}) collective-permute-start(bf16[24,1792]{1,0:T(8,128)(2,1)S(1)} %project.6), channel_id=1, source_target_pairs={{0,8},{4,12},{8,0},{12,4},{1,9},{5,13},{9,1},{13,5},{2,10},{6,14},... | collective-permute-start | bytes 258056 | tf_op jit(solution)/shard_map/ppermute | solution.py:42
  34.0 7.2 %collective-permute-start.12 = (bf16[24,1792]{1,0:T(8,128)(2,1)S(1)}, bf16[24,1792]{1,0:T(8,128)(2,1)S(1)}, u32[]{:S(2)}, u32[]{:S(2)}) collective-permute-start(bf16[24,1792]{1,0:T(8,128)(2,1)S(1)} %project.7), channel_id=1, source_target_pairs={{0,12},{4,8},{8,4},{12,0},{1,13},{5,9},{9,5},{13,1},{2,14},{6,10},... | collective-permute-start | bytes 258056 | tf_op jit(solution)/shard_map/ppermute | solution.py:42

commit v3 on v2

--- a/solution.py
+++ b/solution.py
@@ -224,7 +224,30 @@
     )(after, query, weight, entries, lengths, cache)
 
 
-def update_kernel(chips, *refs):
+def flip_kernel(after, cache, out, done):
+    del after
+    for b in range(cache.shape[0]):
+        out[b] = cache[b, :KL, :].T
+    done[...] = jnp.zeros_like(done)
+
+
+def flip(after, cache):
+    return pl.pallas_call(
+        flip_kernel,
+        out_shape=[
+            jax.ShapeDtypeStruct((cache.shape[0], CACHE, KL), cache.dtype),
+            jax.ShapeDtypeStruct((8, 128), jnp.float32),
+        ],
+        in_specs=[VMEM_SPEC] * 2,
+        out_specs=[VMEM_SPEC] * 2,
+        compiler_params=pltpu.CompilerParams(vmem_limit_bytes=4 << 20),
+        cost_estimate=pl.CostEstimate(flops=4 * 10**9, bytes_accessed=10**6, transcendentals=0),
+        name="flip",
+    )(after, cache)
+
+
+def update_kernel(chips, done, *refs):
+    del done
     total, latents = refs[:2]
     packs, refs = refs[2:chips + 1], refs[chips + 1:]
     states, outs = refs[:6], refs[6:]
@@ -259,7 +282,7 @@
     gives[0][...] = key_half
 
 
-def update(total, latents, packs, states):
+def update(done, total, latents, packs, states):
     chips = len(packs) + 1
     tokens, width = latents.shape
     key_rows = states[3].shape[0]
@@ -271,12 +294,12 @@
             jax.ShapeDtypeStruct((key_rows, width), jnp.bfloat16),
         ]
         + [jax.ShapeDtypeStruct((tokens + key_rows, width), jnp.bfloat16)] * (chips - 1),
-        in_specs=[VMEM_SPEC] * (chips + 7),
+        in_specs=[VMEM_SPEC] * (chips + 8),
         out_specs=[VMEM_SPEC] * (chips + 7),
         compiler_params=pltpu.CompilerParams(vmem_limit_bytes=8 << 20),
         cost_estimate=pl.CostEstimate(flops=4 * 10**9, bytes_accessed=10**6, transcendentals=0),
         name="update",
-    )(total, latents, *packs, *states)
+    )(done, total, latents, *packs, *states)
     return outs[:6], outs[6], outs[7], outs[8:]
 
 
@@ -311,7 +334,7 @@
 
 def attend_kernel(
     rows,
-    query_sum, pair_own, pair_got, query_rope, new_keys, rope_scores, lengths, value_up, cache,
+    query_sum, pair_own, pair_got, query_rope, new_keys, rope_scores, lengths, value_up, cache, flipped,
     out, key_full,
 ):
     f32, bf16 = jnp.float32, jnp.bfloat16
@@ -360,7 +383,7 @@
     latent_out = dot((fresh / denominator).astype(bf16), new_keys[:, :KL], nn)
     for b in range(rows):
         mine = jnp.where(batch_of == b, probs, jnp.zeros_like(probs))
-        latent_out = latent_out + dot(mine, cache[b, :KL, :], nt)
+        latent_out = latent_out + dot(mine, flipped[b], nn)
     latent_out = latent_out.astype(bf16)
     head_values = jnp.concatenate(
         [
@@ -377,20 +400,21 @@
 
 
 def attend(
-    query_sum, pair_own, pair_got, query_rope, new_keys, rope_scores, lengths, value_up, cache
+    query_sum, pair_own, pair_got, query_rope, new_keys, rope_scores, lengths, value_up, cache,
+    flipped,
 ):
     tokens, width = query_sum.shape
     return pl.pallas_call(
         functools.partial(attend_kernel, lengths.shape[0]),
         out_shape=jax.ShapeDtypeStruct((tokens, width), jnp.bfloat16),
-        in_specs=[VMEM_SPEC] * 9,
+        in_specs=[VMEM_SPEC] * 10,
         out_specs=VMEM_SPEC,
         scratch_shapes=[pltpu.VMEM((KL, width), jnp.bfloat16)],
         compiler_params=pltpu.CompilerParams(vmem_limit_bytes=16 << 20),
         name="attend",
     )(
         query_sum, pair_own, pair_got, query_rope, new_keys, rope_scores, lengths[None, :],
-        value_up, cache,
+        value_up, cache, flipped,
     )
 
 
@@ -463,6 +487,7 @@
     own, latent_own = own_blocks(query_grads, key_grads, flat_query)
     total, columns, packs = pack_sums(own, query_got, key_got, latent_own, latent_got)
     cache = latent_cache.transpose(0, 2, 1)
+    flipped, done = flip(columns, cache)
     query_rope, new_keys, rope_scores = rope(
         columns,
         flat_query,
@@ -474,14 +499,14 @@
     packs = [swap(pack, ROW_AXES, devices, 2 * j + 2) for j, pack in enumerate(packs)]
 
     states = (query_up, query_moment, query_second, key_up, key_moment, key_second)
-    states, query_sum, key_half, gives = update(total, columns, packs, states)
+    states, query_sum, key_half, gives = update(done, total, columns, packs, states)
     query_weight, query_first, query_square, key_weight, key_first, key_square = states
     gots = [swap(give, ROW_AXES, devices, 2 * j + 2) for j, give in enumerate(gives)]
     query_sum, pair_own = merge(query_sum, key_half, gots)
     pair_got = swap(pair_own, ROW_AXES, devices, 1)
     head_values = attend(
         query_sum, pair_own, pair_got, query_rope, new_keys, rope_scores, lengths, value_up,
-        cache,
+        cache, flipped,
     )
     attended, *give = project_all(head_values, output_weight)
     shares = lax.axis_size("fsdp")

time: 42 us -> 41.5 us (0.988)
  waiting for transfers between devices: 16.4 us -> 15 us
  Pallas kernels: 6.31 us -> 7.27 us
    ppermute x13, waiting for transfers between devices: 16.4 us -> 15 us  [swap(): return lax.ppermute(value, axes, [(i, i ^ distance) for i in range(count)])]
    pallas_call x0 -> x1, Pallas kernels: none -> 1.13 us  [flip(): pl.pallas_call(flip_kernel, out_shape=[jax.ShapeDtypeStruct((cache.shape[...]
    pallas_call x1, Pallas kernels: 2.78 us -> 2.29 us  [attend(): pl.pallas_call(functools.partial(attend_kernel, lengths.shape[0]), out_sh...]
    unnamed x34 -> x32, local copies, waits for them, and re-layouts: 3.99 us -> 3.98 us
  transfers between devices with their start and end apart: 13 -> 13, of which waited for: 9 -> 9; matrix products, arithmetic and copies ran while one was open for 9% -> 9% of each run, Pallas kernels for 5% -> 9%
where the time goes in v3:
time: 41.5 us; the launch traced here: 41.3 us
  waiting for transfers between devices  15 us (36%)
  starting transfers between devices  13.6 us (33%)
  Pallas kernels  7.27 us (18%)
  local copies, waits for them, and re-layouts  3.98 us (10%)
  between operations  0.82 us (2%)
  other arithmetic  0.69 us (2%)
    ppermute x13, waiting for transfers between devices, swap(): return lax.ppermute(value, axes, [(i, i ^ distance) for i in range(count)])  15 us
    ppermute x13, starting transfers between devices, swap(): return lax.ppermute(value, axes, [(i, i ^ distance) for i in range(count)])  13.6 us
    unnamed x32, local copies, waits for them, and re-layouts  3.98 us
    pallas_call x1, Pallas kernels, attend(): pl.pallas_call(functools.partial(attend_kernel, lengths.shape[0]), out_sh...  2.29 us
    pallas_call x1, Pallas kernels, own_blocks(): pl.pallas_call(own_kernel, out_shape=[jax.ShapeDtypeStruct((chips, grad_r...  1.54 us
    pallas_call x4, Pallas kernels, project(): pl.pallas_call(functools.partial(project_kernel, distance), out_shape=jax...  1.14 us
    pallas_call x1, Pallas kernels, flip(): pl.pallas_call(flip_kernel, out_shape=[jax.ShapeDtypeStruct((cache.shape[...  1.13 us
  transfers between devices with their start and end apart: 13, of which 9 were waited for; matrix products, arithmetic and copies ran while one was open for 9% of the time, Pallas kernels for 9%

profile of v3, /device:TPU:0, one launch (start us, length us, event | category | flops | bytes accessed | tf_op | source)
XLA Modules:
  0.0 41.3 jit_solution(12282879885265790066)
XLA Ops:
  0.6 0.0 copy-start.1
  0.6 0.6 %collective-permute-start = (bf16[1536,256]{1,0:T(8,128)(2,1)}, bf16[1536,256]{1,0:T(8,128)(2,1)S(1)}, u32[]{:S(2)}, u32[]{:S(2)}) collective-permute-start(bf16[1536,256]{1,0:T(8,128)(2,1)} %query_own.1), channel_id=1, source_target_pairs={{0,1},{1,0},{2,3},{3,2},{16,17},{17,16},{18,19},{19,18},{4,5},{5,4... | collective-permute-start | bytes 2359304 | tf_op jit(solution)/shard_map/ppermute | solution.py:42
  1.2 0.1 collective-permute-start.1
  1.3 0.4 %collective-permute-start.2 = (bf16[24,1536]{1,0:T(8,128)(2,1)}, bf16[24,1536]{1,0:T(8,128)(2,1)S(1)}, u32[]{:S(2)}, u32[]{:S(2)}) collective-permute-start(bf16[24,1536]{1,0:T(8,128)(2,1)} %bitcast.13), channel_id=1, source_target_pairs={{0,1},{1,0},{2,3},{3,2},{16,17},{17,16},{18,19},{19,18},{4,5},{5,4... | collective-permute-start | bytes 221192 | tf_op jit(solution)/shard_map/ppermute | solution.py:42
  1.7 1.5 %own.1 = (bf16[4,256,256]{2,1,0:T(8,128)(2,1)S(1)}, bf16[4,24,256]{2,1,0:T(8,128)(2,1)S(1)}) custom-call(bf16[1536,256]{1,0:T(8,128)(2,1)} %query_own.1, bf16[512,256]{1,0:T(8,128)(2,1)} %key_own.1, bf16[24,1536]{1,0:T(8,128)(2,1)} %bitcast.14), custom_call_target="tpu_custom_call" | custom-call | flops 1000000000 | bytes 1000000 | tf_op jit(solution)/shard_map/own/pallas_call | solution.py:106
  3.3 0.5 %collective-permute-done.2.latents = bf16[24,1536]{1,0:T(8,128)(2,1)S(1)} collective-permute-done((bf16[24,1536]{1,0:T(8,128)(2,1)}, bf16[24,1536]{1,0:T(8,128)(2,1)S(1)}, u32[]{:S(2)}, u32[]{:S(2)}) %collective-permute-start.2) | collective-permute-done | bytes 73760 | tf_op jit(solution)/shard_map/ppermute | solution.py:42
  3.8 0.0 collective-permute-done.1.key_got
  3.8 0.0 collective-permute-done.query_got
  3.8 0.2 pack.1
  4.0 2.9 %collective-permute-start.3 = (bf16[304,256]{1,0:T(8,128)(2,1)S(1)}, bf16[304,256]{1,0:T(8,128)(2,1)S(1)}, u32[]{:S(2)}, u32[]{:S(2)}) collective-permute-start(bf16[304,256]{1,0:T(8,128)(2,1)S(1)} %get-tuple-element.37), channel_id=1, source_target_pairs={{0,2},{1,3},{2,0},{3,1},{16,18},{17,19},{18,16},{19,17},{4,6},{5,7... | collective-permute-start | bytes 466952 | tf_op jit(solution)/shard_map/ppermute | solution.py:42
  6.9 1.5 %collective-permute-start.4 = (bf16[304,256]{1,0:T(8,128)(2,1)S(1)}, bf16[304,256]{1,0:T(8,128)(2,1)S(1)}, u32[]{:S(2)}, u32[]{:S(2)}) collective-permute-start(bf16[304,256]{1,0:T(8,128)(2,1)S(1)} %get-tuple-element.38), channel_id=1, source_target_pairs={{0,16},{1,17},{2,18},{3,19},{16,0},{17,1},{18,2},{19,3},{4,20},{5,... | collective-permute-start | bytes 466952 | tf_op jit(solution)/shard_map/ppermute | solution.py:42
  8.4 0.1 collective-permute-start.5
  8.5 0.0 copy-done.1
  8.5 0.0 copy-start.10
  8.5 0.0 copy-start.11
  8.5 0.0 copy-start.12
  8.5 1.1 %flip.1 = (bf16[8,512,512]{2,1,0:T(8,128)(2,1)S(1)}, f32[8,128]{1,0:T(8,128)S(1)}) custom-call(bf16[48,256]{1,0:T(8,128)(2,1)S(1)} %get-tuple-element.34.after.refs_1_, bf16[8,576,512]{2,1,0:T(8,128)(2,1)S(1)} %bitcast.10), custom_call_target="tpu_custom_call" | custom-call | flops 4000000000 | bytes 1000000 | tf_op jit(solution)/shard_map/flip/pallas_call | solution.py:235
  9.7 1.6 %collective-permute-done.3.refs_2_ = bf16[304,256]{1,0:T(8,128)(2,1)S(1)} collective-permute-done((bf16[304,256]{1,0:T(8,128)(2,1)S(1)}, bf16[304,256]{1,0:T(8,128)(2,1)S(1)}, u32[]{:S(2)}, u32[]{:S(2)}) %collective-permute-start.3) | collective-permute-done | bytes 155680 | tf_op jit(solution)/shard_map/ppermute | solution.py:42
  11.3 2.6 %collective-permute-done.4.refs_3_ = bf16[304,256]{1,0:T(8,128)(2,1)S(1)} collective-permute-done((bf16[304,256]{1,0:T(8,128)(2,1)S(1)}, bf16[304,256]{1,0:T(8,128)(2,1)S(1)}, u32[]{:S(2)}, u32[]{:S(2)}) %collective-permute-start.4) | collective-permute-done | bytes 155680 | tf_op jit(solution)/shard_map/ppermute | solution.py:42
  13.8 2.0 %collective-permute-done.5.refs_4_ = bf16[304,256]{1,0:T(8,128)(2,1)S(1)} collective-permute-done((bf16[304,256]{1,0:T(8,128)(2,1)S(1)}, bf16[304,256]{1,0:T(8,128)(2,1)S(1)}, u32[]{:S(2)}, u32[]{:S(2)}) %collective-permute-start.5) | collective-permute-done | bytes 155680 | tf_op jit(solution)/shard_map/ppermute | solution.py:42
  15.9 0.0 copy-done.7
  15.9 0.0 copy-done.8
  15.9 0.0 copy-done.9
  15.9 0.0 copy-done.10
  15.9 0.0 copy-done.11
  15.9 0.0 copy-done.12
  15.9 0.0 copy-start.2
  15.9 0.0 copy-start.4
  15.9 0.0 copy-start.5
  15.9 0.0 copy-start.6
  15.9 0.4 update.1
  16.3 0.0 copy-start.3
  16.3 1.7 %collective-permute-start.6 = (bf16[112,256]{1,0:T(8,128)(2,1)S(1)}, bf16[112,256]{1,0:T(8,128)(2,1)S(1)}, u32[]{:S(2)}, u32[]{:S(2)}) collective-permute-start(bf16[112,256]{1,0:T(8,128)(2,1)S(1)} %get-tuple-element.48), channel_id=1, source_target_pairs={{0,2},{1,3},{2,0},{3,1},{16,18},{17,19},{18,16},{19,17},{4,6},{5,7... | collective-permute-start | bytes 172040 | tf_op jit(solution)/shard_map/ppermute | solution.py:42
  18.1 1.5 %collective-permute-start.7 = (bf16[112,256]{1,0:T(8,128)(2,1)S(1)}, bf16[112,256]{1,0:T(8,128)(2,1)S(1)}, u32[]{:S(2)}, u32[]{:S(2)}) collective-permute-start(bf16[112,256]{1,0:T(8,128)(2,1)S(1)} %get-tuple-element.49), channel_id=1, source_target_pairs={{0,16},{1,17},{2,18},{3,19},{16,0},{17,1},{18,2},{19,3},{4,20},{5,... | collective-permute-start | bytes 172040 | tf_op jit(solution)/shard_map/ppermute | solution.py:42
  19.6 0.3 collective-permute-start.8
  19.9 0.7 %collective-permute-done.6.refs_0_ = bf16[112,256]{1,0:T(8,128)(2,1)S(1)} collective-permute-done((bf16[112,256]{1,0:T(8,128)(2,1)S(1)}, bf16[112,256]{1,0:T(8,128)(2,1)S(1)}, u32[]{:S(2)}, u32[]{:S(2)}) %collective-permute-start.6) | collective-permute-done | bytes 57376 | tf_op jit(solution)/shard_map/ppermute | solution.py:42
  20.6 1.7 %collective-permute-done.7.refs_1_ = bf16[112,256]{1,0:T(8,128)(2,1)S(1)} collective-permute-done((bf16[112,256]{1,0:T(8,128)(2,1)S(1)}, bf16[112,256]{1,0:T(8,128)(2,1)S(1)}, u32[]{:S(2)}, u32[]{:S(2)}) %collective-permute-start.7) | collective-permute-done | bytes 57376 | tf_op jit(solution)/shard_map/ppermute | solution.py:42
  22.2 2.4 %collective-permute-done.8.refs_2_ = bf16[112,256]{1,0:T(8,128)(2,1)S(1)} collective-permute-done((bf16[112,256]{1,0:T(8,128)(2,1)S(1)}, bf16[112,256]{1,0:T(8,128)(2,1)S(1)}, u32[]{:S(2)}, u32[]{:S(2)}) %collective-permute-start.8) | collective-permute-done | bytes 57376 | tf_op jit(solution)/shard_map/ppermute | solution.py:42
  24.7 0.1 collective-permute-start.9
  24.7 0.0 copy-done.2
  24.7 0.0 copy-done.4
  24.8 0.0 copy-done.5
  24.8 0.0 copy-done.6
  24.8 0.6 %rope.1 = (bf16[48,64]{1,0:T(8,128)(2,1)S(1)}, bf16[24,576]{1,0:T(8,128)(2,1)S(1)}, f32[48,512]{1,0:T(8,128)S(1)}) custom-call(bf16[48,256]{1,0:T(8,128)(2,1)S(1)} %get-tuple-element.34.after.refs_1_, bf16[24,1536]{1,0:T(8,128)(2,1)S(1)} %bitcast.15, bf16[1536,128]{1,0:T(8,128)(2,1)S(1)} %copy-done.2, bf16[24,576]{1,0:T(8,128)(2,1)S(1)} %bitcast.16, ...), custom_call_target="tpu_custom_call" | custom-call | tf_op jit(solution)/shard_map/rope/pallas_call | solution.py:213
  25.4 0.7 %collective-permute-done.9.pair_got = bf16[280,256]{1,0:T(8,128)(2,1)S(1)} collective-permute-done((bf16[280,256]{1,0:T(8,128)(2,1)S(1)}, bf16[280,256]{1,0:T(8,128)(2,1)S(1)}, u32[]{:S(2)}, u32[]{:S(2)}) %collective-permute-start.9) | collective-permute-done | bytes 143392 | tf_op jit(solution)/shard_map/ppermute | solution.py:42
  26.1 0.0 copy-done.3
  26.1 2.3 %attend.1.head_values = bf16[24,256]{1,0:T(8,128)(2,1)S(1)} custom-call(f32[24,256]{1,0:T(8,128)S(1)} %get-tuple-element.51.query_sum, bf16[280,256]{1,0:T(8,128)(2,1)S(1)} %get-tuple-element.52.pair_own, bf16[280,256]{1,0:T(8,128)(2,1)S(1)} %collective-permute-done.9.pair_got, bf16[48,64]{1,0:T(8,128)(2,1)S(1)} %get-tuple-element.53.query_rope, ...), custom_call_target="tpu_custom_call" | custom-call | tf_op jit(solution)/shard_map/attend/pallas_call | solution.py:407
  28.4 0.3 project.5
  28.7 0.3 project.6
  29.0 0.3 project.7
  29.3 1.6 %collective-permute-start.10 = (bf16[24,1792]{1,0:T(8,128)(2,1)S(1)}, bf16[24,1792]{1,0:T(8,128)(2,1)S(1)}, u32[]{:S(2)}, u32[]{:S(2)}) collective-permute-start(bf16[24,1792]{1,0:T(8,128)(2,1)S(1)} %project.5), channel_id=1, source_target_pairs={{0,4},{4,0},{8,12},{12,8},{1,5},{5,1},{9,13},{13,9},{2,6},{6,2},{1... | collective-permute-start | bytes 258056 | tf_op jit(solution)/shard_map/ppermute | solution.py:42
  30.9 2.6 %collective-permute-start.11 = (bf16[24,1792]{1,0:T(8,128)(2,1)S(1)}, bf16[24,1792]{1,0:T(8,128)(2,1)S(1)}, u32[]{:S(2)}, u32[]{:S(2)}) collective-permute-start(bf16[24,1792]{1,0:T(8,128)(2,1)S(1)} %project.6), channel_id=1, source_target_pairs={{0,8},{4,12},{8,0},{12,4},{1,9},{5,13},{9,1},{13,5},{2,10},{6,14},... | collective-permute-start | bytes 258056 | tf_op jit(solution)/shard_map/ppermute | solution.py:42
  33.5 0.2 collective-permute-start.12
  33.7 0.7 %copy.22 = f32[192,256]{1,0:T(8,128)} copy(f32[192,256]{1,0:T(8,128)S(1)} %get-tuple-element.57) | data formatting | bytes 393216
  34.3 0.7 %copy.24 = f32[192,256]{1,0:T(8,128)} copy(f32[192,256]{1,0:T(8,128)S(1)} %get-tuple-element.59) | data formatting | bytes 393216
  35.0 0.7 %copy.25 = f32[192,256]{1,0:T(8,128)} copy(f32[192,256]{1,0:T(8,128)S(1)} %get-tuple-element.60) | data formatting | bytes 393216
  35.7 0.6 %copy.23 = f32[64,256]{1,0:T(8,128)} copy(f32[64,256]{1,0:T(8,128)S(1)} %get-tuple-element.58) | data formatting | bytes 131072
  36.3 0.6 %copy.26 = f32[64,256]{1,0:T(8,128)} copy(f32[64,256]{1,0:T(8,128)S(1)} %get-tuple-element.61) | data formatting | bytes 131072
  37.0 0.6 %copy.27 = f32[64,256]{1,0:T(8,128)} copy(f32[64,256]{1,0:T(8,128)S(1)} %get-tuple-element.62) | data formatting | bytes 131072
  37.6 0.3 project.4
  37.9 0.0 collective-permute-done.10
  37.9 2.8 %collective-permute-done.11 = bf16[24,1792]{1,0:T(8,128)(2,1)S(1)} collective-permute-done((bf16[24,1792]{1,0:T(8,128)(2,1)S(1)}, bf16[24,1792]{1,0:T(8,128)(2,1)S(1)}, u32[]{:S(2)}, u32[]{:S(2)}) %collective-permute-start.11) | collective-permute-done | bytes 86048 | tf_op jit(solution)/shard_map/ppermute | solution.py:42
  40.6 0.0 collective-permute-done.12
  40.6 0.7 %fusion = bf16[1792,24]{0,1:T(8,128)(2,1)} fusion(bf16[24,1792]{1,0:T(8,128)(2,1)S(1)} %collective-permute-done.12, bf16[24,1792]{1,0:T(8,128)(2,1)S(1)} %collective-permute-done.11, f32[24,1792]{1,0:T(8,128)S(1)} %project.4, bf16[24,1792]{1,0:T(8,128)(2,1)S(1)} %collective-permute-done.10), kind=kLoop, calls=%fused_computation.1 | loop fusion | flops 301056 | bytes 516096 | tf_op jit(solution)/shard_map/transpose | solution.py:516
  (6 shorter events, 0.0 us)
Async XLA Ops:
  0.6 7.8 %copy-start.1 = (bf16[8,512,576]{1,2,0:T(8,128)(2,1)S(1)}, bf16[8,512,576]{1,2,0:T(8,128)(2,1)}, u32[]{:S(2)}) copy-start(bf16[8,512,576]{1,2,0:T(8,128)(2,1)} %param.17) | copy-start | bytes 14155780
  0.6 3.2 %collective-permute-start = (bf16[1536,256]{1,0:T(8,128)(2,1)}, bf16[1536,256]{1,0:T(8,128)(2,1)S(1)}, u32[]{:S(2)}, u32[]{:S(2)}) collective-permute-start(bf16[1536,256]{1,0:T(8,128)(2,1)} %query_own.1), channel_id=1, source_target_pairs={{0,1},{1,0},{2,3},{3,2},{16,17},{17,16},{18,19},{19,18},{4,5},{5,4... | collective-permute-start | bytes 2359304 | tf_op jit(solution)/shard_map/ppermute | solution.py:42
  1.2 2.6 %collective-permute-start.1 = (bf16[512,256]{1,0:T(8,128)(2,1)}, bf16[512,256]{1,0:T(8,128)(2,1)S(1)}, u32[]{:S(2)}, u32[]{:S(2)}) collective-permute-start(bf16[512,256]{1,0:T(8,128)(2,1)} %key_own.1), channel_id=1, source_target_pairs={{0,1},{1,0},{2,3},{3,2},{16,17},{17,16},{18,19},{19,18},{4,5},{5,4... | collective-permute-start | bytes 786440 | tf_op jit(solution)/shard_map/ppermute | solution.py:42
  1.3 2.5 %collective-permute-start.2 = (bf16[24,1536]{1,0:T(8,128)(2,1)}, bf16[24,1536]{1,0:T(8,128)(2,1)S(1)}, u32[]{:S(2)}, u32[]{:S(2)}) collective-permute-start(bf16[24,1536]{1,0:T(8,128)(2,1)} %bitcast.13), channel_id=1, source_target_pairs={{0,1},{1,0},{2,3},{3,2},{16,17},{17,16},{18,19},{19,18},{4,5},{5,4... | collective-permute-start | bytes 221192 | tf_op jit(solution)/shard_map/ppermute | solution.py:42
  4.0 7.3 %collective-permute-start.3 = (bf16[304,256]{1,0:T(8,128)(2,1)S(1)}, bf16[304,256]{1,0:T(8,128)(2,1)S(1)}, u32[]{:S(2)}, u32[]{:S(2)}) collective-permute-start(bf16[304,256]{1,0:T(8,128)(2,1)S(1)} %get-tuple-element.37), channel_id=1, source_target_pairs={{0,2},{1,3},{2,0},{3,1},{16,18},{17,19},{18,16},{19,17},{4,6},{5,7... | collective-permute-start | bytes 466952 | tf_op jit(solution)/shard_map/ppermute | solution.py:42
  6.9 6.9 %collective-permute-start.4 = (bf16[304,256]{1,0:T(8,128)(2,1)S(1)}, bf16[304,256]{1,0:T(8,128)(2,1)S(1)}, u32[]{:S(2)}, u32[]{:S(2)}) collective-permute-start(bf16[304,256]{1,0:T(8,128)(2,1)S(1)} %get-tuple-element.38), channel_id=1, source_target_pairs={{0,16},{1,17},{2,18},{3,19},{16,0},{17,1},{18,2},{19,3},{4,20},{5,... | collective-permute-start | bytes 466952 | tf_op jit(solution)/shard_map/ppermute | solution.py:42
  8.4 7.4 %collective-permute-start.5 = (bf16[304,256]{1,0:T(8,128)(2,1)S(1)}, bf16[304,256]{1,0:T(8,128)(2,1)S(1)}, u32[]{:S(2)}, u32[]{:S(2)}) collective-permute-start(bf16[304,256]{1,0:T(8,128)(2,1)S(1)} %get-tuple-element.39), channel_id=1, source_target_pairs={{0,18},{1,19},{2,16},{3,17},{16,2},{17,3},{18,0},{19,1},{4,22},{5,... | collective-permute-start | bytes 466952 | tf_op jit(solution)/shard_map/ppermute | solution.py:42
  8.5 7.4 %copy-start.7 = (f32[192,256]{1,0:T(8,128)S(1)}, f32[192,256]{1,0:T(8,128)}, u32[]{:S(2)}) copy-start(f32[192,256]{1,0:T(8,128)} %refs_5_.1) | copy-start | bytes 589828
  8.5 7.4 %copy-start.8 = (f32[192,256]{1,0:T(8,128)S(1)}, f32[192,256]{1,0:T(8,128)}, u32[]{:S(2)}) copy-start(f32[192,256]{1,0:T(8,128)} %refs_6_.1) | copy-start | bytes 589828
  8.5 7.4 %copy-start.9 = (f32[192,256]{1,0:T(8,128)S(1)}, f32[192,256]{1,0:T(8,128)}, u32[]{:S(2)}) copy-start(f32[192,256]{1,0:T(8,128)} %refs_7_.1) | copy-start | bytes 589828
  8.5 7.4 %copy-start.10 = (f32[64,256]{1,0:T(8,128)S(1)}, f32[64,256]{1,0:T(8,128)}, u32[]{:S(2)}) copy-start(f32[64,256]{1,0:T(8,128)} %refs_8_.1) | copy-start | bytes 196612
  8.5 7.4 %copy-start.11 = (f32[64,256]{1,0:T(8,128)S(1)}, f32[64,256]{1,0:T(8,128)}, u32[]{:S(2)}) copy-start(f32[64,256]{1,0:T(8,128)} %refs_9_.1) | copy-start | bytes 196612
  8.5 7.4 %copy-start.12 = (f32[64,256]{1,0:T(8,128)S(1)}, f32[64,256]{1,0:T(8,128)}, u32[]{:S(2)}) copy-start(f32[64,256]{1,0:T(8,128)} %refs_10_.1) | copy-start | bytes 196612
  15.9 8.8 %copy-start.2 = (bf16[1536,128]{1,0:T(8,128)(2,1)S(1)}, bf16[1536,128]{1,0:T(8,128)(2,1)}, u32[]{:S(2)}) copy-start(bf16[1536,128]{1,0:T(8,128)(2,1)} %weight.5) | copy-start | bytes 1179652
  15.9 8.8 %copy-start.4 = (bf16[8,3,1536]{2,0,1:T(8,128)(2,1)S(1)}, bf16[8,3,1536]{2,0,1:T(8,128)(2,1)}, u32[]{:S(2)}) copy-start(bf16[8,3,1536]{2,0,1:T(8,128)(2,1)} %param.15) | copy-start | bytes 221188
  15.9 8.8 %copy-start.5 = (bf16[8,3,576]{2,0,1:T(8,128)(2,1)S(1)}, bf16[8,3,576]{2,0,1:T(8,128)(2,1)}, u32[]{:S(2)}) copy-start(bf16[8,3,576]{2,0,1:T(8,128)(2,1)} %param.16) | copy-start | bytes 82948
  15.9 8.8 %copy-start.6 = (s32[8]{0:T(128)S(1)}, s32[8]{0:T(128)}, u32[]{:S(2)}) copy-start(s32[8]{0:T(128)} %param.18) | copy-start | bytes 100
  16.3 9.8 %copy-start.3 = (bf16[512,256]{1,0:T(8,128)(2,1)S(1)}, bf16[512,256]{1,0:T(8,128)(2,1)}, u32[]{:S(2)}) copy-start(bf16[512,256]{1,0:T(8,128)(2,1)} %value_up.1) | copy-start | bytes 786436
  16.3 4.2 %collective-permute-start.6 = (bf16[112,256]{1,0:T(8,128)(2,1)S(1)}, bf16[112,256]{1,0:T(8,128)(2,1)S(1)}, u32[]{:S(2)}, u32[]{:S(2)}) collective-permute-start(bf16[112,256]{1,0:T(8,128)(2,1)S(1)} %get-tuple-element.48), channel_id=1, source_target_pairs={{0,2},{1,3},{2,0},{3,1},{16,18},{17,19},{18,16},{19,17},{4,6},{5,7... | collective-permute-start | bytes 172040 | tf_op jit(solution)/shard_map/ppermute | solution.py:42
  18.1 4.2 %collective-permute-start.7 = (bf16[112,256]{1,0:T(8,128)(2,1)S(1)}, bf16[112,256]{1,0:T(8,128)(2,1)S(1)}, u32[]{:S(2)}, u32[]{:S(2)}) collective-permute-start(bf16[112,256]{1,0:T(8,128)(2,1)S(1)} %get-tuple-element.49), channel_id=1, source_target_pairs={{0,16},{1,17},{2,18},{3,19},{16,0},{17,1},{18,2},{19,3},{4,20},{5,... | collective-permute-start | bytes 172040 | tf_op jit(solution)/shard_map/ppermute | solution.py:42
  19.6 5.1 %collective-permute-start.8 = (bf16[112,256]{1,0:T(8,128)(2,1)S(1)}, bf16[112,256]{1,0:T(8,128)(2,1)S(1)}, u32[]{:S(2)}, u32[]{:S(2)}) collective-permute-start(bf16[112,256]{1,0:T(8,128)(2,1)S(1)} %get-tuple-element.50), channel_id=1, source_target_pairs={{0,18},{1,19},{2,16},{3,17},{16,2},{17,3},{18,0},{19,1},{4,22},{5,... | collective-permute-start | bytes 172040 | tf_op jit(solution)/shard_map/ppermute | solution.py:42
  24.7 1.4 %collective-permute-start.9 = (bf16[280,256]{1,0:T(8,128)(2,1)S(1)}, bf16[280,256]{1,0:T(8,128)(2,1)S(1)}, u32[]{:S(2)}, u32[]{:S(2)}) collective-permute-start(bf16[280,256]{1,0:T(8,128)(2,1)S(1)} %get-tuple-element.52.pair_own), channel_id=1, source_target_pairs={{0,1},{1,0},{2,3},{3,2},{16,17},{17,16},{18,19},{19,18},{4,5},{5,4... | collective-permute-start | bytes 430088 | tf_op jit(solution)/shard_map/ppermute | solution.py:42
  26.1 2.3 %copy-start = (bf16[256,7168]{1,0:T(8,128)(2,1)S(1)}, bf16[256,7168]{1,0:T(8,128)(2,1)}, u32[]{:S(2)}) copy-start(bf16[256,7168]{1,0:T(8,128)(2,1)} %weight.9) | copy-start | bytes 11010052
  29.3 8.6 %collective-permute-start.10 = (bf16[24,1792]{1,0:T(8,128)(2,1)S(1)}, bf16[24,1792]{1,0:T(8,128)(2,1)S(1)}, u32[]{:S(2)}, u32[]{:S(2)}) collective-permute-start(bf16[24,1792]{1,0:T(8,128)(2,1)S(1)} %project.5), channel_id=1, source_target_pairs={{0,4},{4,0},{8,12},{12,8},{1,5},{5,1},{9,13},{13,9},{2,6},{6,2},{1... | collective-permute-start | bytes 258056 | tf_op jit(solution)/shard_map/ppermute | solution.py:42
  30.9 9.8 %collective-permute-start.11 = (bf16[24,1792]{1,0:T(8,128)(2,1)S(1)}, bf16[24,1792]{1,0:T(8,128)(2,1)S(1)}, u32[]{:S(2)}, u32[]{:S(2)}) collective-permute-start(bf16[24,1792]{1,0:T(8,128)(2,1)S(1)} %project.6), channel_id=1, source_target_pairs={{0,8},{4,12},{8,0},{12,4},{1,9},{5,13},{9,1},{13,5},{2,10},{6,14},... | collective-permute-start | bytes 258056 | tf_op jit(solution)/shard_map/ppermute | solution.py:42
  33.5 7.2 %collective-permute-start.12 = (bf16[24,1792]{1,0:T(8,128)(2,1)S(1)}, bf16[24,1792]{1,0:T(8,128)(2,1)S(1)}, u32[]{:S(2)}, u32[]{:S(2)}) collective-permute-start(bf16[24,1792]{1,0:T(8,128)(2,1)S(1)} %project.7), channel_id=1, source_target_pairs={{0,12},{4,8},{8,4},{12,0},{1,13},{5,9},{9,5},{13,1},{2,14},{6,10},... | collective-permute-start | bytes 258056 | tf_op jit(solution)/shard_map/ppermute | solution.py:42

commit v4 on v3

--- a/solution.py
+++ b/solution.py
@@ -379,8 +379,9 @@
     )
     scores, fresh = jnp.exp(scores - highest), jnp.exp(fresh - highest)
     denominator = jnp.sum(scores, -1, keepdims=True) + jnp.sum(fresh, -1, keepdims=True)
-    probs = (scores / denominator).astype(bf16)
-    latent_out = dot((fresh / denominator).astype(bf16), new_keys[:, :KL], nn)
+    inverse = 1.0 / denominator
+    probs = (scores * inverse).astype(bf16)
+    latent_out = dot((fresh * inverse).astype(bf16), new_keys[:, :KL], nn)
     for b in range(rows):
         mine = jnp.where(batch_of == b, probs, jnp.zeros_like(probs))
         latent_out = latent_out + dot(mine, flipped[b], nn)

time: 41.5 us -> 41.5 us (level)
  no operation moved by 1% of the time
where the time goes in v4:
time: 41.5 us; the launch traced here: 41.3 us
  waiting for transfers between devices  15 us (36%)
  starting transfers between devices  13.6 us (33%)
  Pallas kernels  7.27 us (18%)
  local copies, waits for them, and re-layouts  3.98 us (10%)
  between operations  0.82 us (2%)
  other arithmetic  0.69 us (2%)
    ppermute x13, waiting for transfers between devices, swap(): return lax.ppermute(value, axes, [(i, i ^ distance) for i in range(count)])  15 us
    ppermute x13, starting transfers between devices, swap(): return lax.ppermute(value, axes, [(i, i ^ distance) for i in range(count)])  13.6 us
    unnamed x32, local copies, waits for them, and re-layouts  3.98 us
    pallas_call x1, Pallas kernels, attend(): pl.pallas_call(functools.partial(attend_kernel, lengths.shape[0]), out_sh...  2.29 us
    pallas_call x1, Pallas kernels, own_blocks(): pl.pallas_call(own_kernel, out_shape=[jax.ShapeDtypeStruct((chips, grad_r...  1.54 us
    pallas_call x4, Pallas kernels, project(): pl.pallas_call(functools.partial(project_kernel, distance), out_shape=jax...  1.14 us
    pallas_call x1, Pallas kernels, flip(): pl.pallas_call(flip_kernel, out_shape=[jax.ShapeDtypeStruct((cache.shape[...  1.13 us
  transfers between devices with their start and end apart: 13, of which 9 were waited for; matrix products, arithmetic and copies ran while one was open for 9% of the time, Pallas kernels for 9%

profile of v4, /device:TPU:0, one launch (start us, length us, event | category | flops | bytes accessed | tf_op | source)
XLA Modules:
  0.0 41.3 jit_solution(12282879885265790066)
XLA Ops:
  0.6 0.0 copy-start.1
  0.6 0.6 %collective-permute-start = (bf16[1536,256]{1,0:T(8,128)(2,1)}, bf16[1536,256]{1,0:T(8,128)(2,1)S(1)}, u32[]{:S(2)}, u32[]{:S(2)}) collective-permute-start(bf16[1536,256]{1,0:T(8,128)(2,1)} %query_own.1), channel_id=1, source_target_pairs={{0,1},{1,0},{2,3},{3,2},{16,17},{17,16},{18,19},{19,18},{4,5},{5,4... | collective-permute-start | bytes 2359304 | tf_op jit(solution)/shard_map/ppermute | solution.py:42
  1.2 0.1 collective-permute-start.1
  1.3 0.4 %collective-permute-start.2 = (bf16[24,1536]{1,0:T(8,128)(2,1)}, bf16[24,1536]{1,0:T(8,128)(2,1)S(1)}, u32[]{:S(2)}, u32[]{:S(2)}) collective-permute-start(bf16[24,1536]{1,0:T(8,128)(2,1)} %bitcast.13), channel_id=1, source_target_pairs={{0,1},{1,0},{2,3},{3,2},{16,17},{17,16},{18,19},{19,18},{4,5},{5,4... | collective-permute-start | bytes 221192 | tf_op jit(solution)/shard_map/ppermute | solution.py:42
  1.7 1.5 %own.1 = (bf16[4,256,256]{2,1,0:T(8,128)(2,1)S(1)}, bf16[4,24,256]{2,1,0:T(8,128)(2,1)S(1)}) custom-call(bf16[1536,256]{1,0:T(8,128)(2,1)} %query_own.1, bf16[512,256]{1,0:T(8,128)(2,1)} %key_own.1, bf16[24,1536]{1,0:T(8,128)(2,1)} %bitcast.14), custom_call_target="tpu_custom_call" | custom-call | flops 1000000000 | bytes 1000000 | tf_op jit(solution)/shard_map/own/pallas_call | solution.py:106
  3.3 0.5 %collective-permute-done.2.latents = bf16[24,1536]{1,0:T(8,128)(2,1)S(1)} collective-permute-done((bf16[24,1536]{1,0:T(8,128)(2,1)}, bf16[24,1536]{1,0:T(8,128)(2,1)S(1)}, u32[]{:S(2)}, u32[]{:S(2)}) %collective-permute-start.2) | collective-permute-done | bytes 73760 | tf_op jit(solution)/shard_map/ppermute | solution.py:42
  3.8 0.0 collective-permute-done.1.key_got
  3.8 0.0 collective-permute-done.query_got
  3.8 0.2 pack.1
  4.0 2.9 %collective-permute-start.3 = (bf16[304,256]{1,0:T(8,128)(2,1)S(1)}, bf16[304,256]{1,0:T(8,128)(2,1)S(1)}, u32[]{:S(2)}, u32[]{:S(2)}) collective-permute-start(bf16[304,256]{1,0:T(8,128)(2,1)S(1)} %get-tuple-element.37), channel_id=1, source_target_pairs={{0,2},{1,3},{2,0},{3,1},{16,18},{17,19},{18,16},{19,17},{4,6},{5,7... | collective-permute-start | bytes 466952 | tf_op jit(solution)/shard_map/ppermute | solution.py:42
  6.9 1.5 %collective-permute-start.4 = (bf16[304,256]{1,0:T(8,128)(2,1)S(1)}, bf16[304,256]{1,0:T(8,128)(2,1)S(1)}, u32[]{:S(2)}, u32[]{:S(2)}) collective-permute-start(bf16[304,256]{1,0:T(8,128)(2,1)S(1)} %get-tuple-element.38), channel_id=1, source_target_pairs={{0,16},{1,17},{2,18},{3,19},{16,0},{17,1},{18,2},{19,3},{4,20},{5,... | collective-permute-start | bytes 466952 | tf_op jit(solution)/shard_map/ppermute | solution.py:42
  8.4 0.1 collective-permute-start.5
  8.5 0.0 copy-done.1
  8.5 0.0 copy-start.10
  8.5 0.0 copy-start.11
  8.5 0.0 copy-start.12
  8.5 1.1 %flip.1 = (bf16[8,512,512]{2,1,0:T(8,128)(2,1)S(1)}, f32[8,128]{1,0:T(8,128)S(1)}) custom-call(bf16[48,256]{1,0:T(8,128)(2,1)S(1)} %get-tuple-element.34.after.refs_1_, bf16[8,576,512]{2,1,0:T(8,128)(2,1)S(1)} %bitcast.10), custom_call_target="tpu_custom_call" | custom-call | flops 4000000000 | bytes 1000000 | tf_op jit(solution)/shard_map/flip/pallas_call | solution.py:235
  9.7 1.6 %collective-permute-done.3.refs_2_ = bf16[304,256]{1,0:T(8,128)(2,1)S(1)} collective-permute-done((bf16[304,256]{1,0:T(8,128)(2,1)S(1)}, bf16[304,256]{1,0:T(8,128)(2,1)S(1)}, u32[]{:S(2)}, u32[]{:S(2)}) %collective-permute-start.3) | collective-permute-done | bytes 155680 | tf_op jit(solution)/shard_map/ppermute | solution.py:42
  11.3 2.6 %collective-permute-done.4.refs_3_ = bf16[304,256]{1,0:T(8,128)(2,1)S(1)} collective-permute-done((bf16[304,256]{1,0:T(8,128)(2,1)S(1)}, bf16[304,256]{1,0:T(8,128)(2,1)S(1)}, u32[]{:S(2)}, u32[]{:S(2)}) %collective-permute-start.4) | collective-permute-done | bytes 155680 | tf_op jit(solution)/shard_map/ppermute | solution.py:42
  13.8 2.0 %collective-permute-done.5.refs_4_ = bf16[304,256]{1,0:T(8,128)(2,1)S(1)} collective-permute-done((bf16[304,256]{1,0:T(8,128)(2,1)S(1)}, bf16[304,256]{1,0:T(8,128)(2,1)S(1)}, u32[]{:S(2)}, u32[]{:S(2)}) %collective-permute-start.5) | collective-permute-done | bytes 155680 | tf_op jit(solution)/shard_map/ppermute | solution.py:42
  15.9 0.0 copy-done.7
  15.9 0.0 copy-done.8
  15.9 0.0 copy-done.9
  15.9 0.0 copy-done.10
  15.9 0.0 copy-done.11
  15.9 0.0 copy-done.12
  15.9 0.0 copy-start.2
  15.9 0.0 copy-start.4
  15.9 0.0 copy-start.5
  15.9 0.0 copy-start.6
  15.9 0.4 update.1
  16.3 0.0 copy-start.3
  16.3 1.7 %collective-permute-start.6 = (bf16[112,256]{1,0:T(8,128)(2,1)S(1)}, bf16[112,256]{1,0:T(8,128)(2,1)S(1)}, u32[]{:S(2)}, u32[]{:S(2)}) collective-permute-start(bf16[112,256]{1,0:T(8,128)(2,1)S(1)} %get-tuple-element.48), channel_id=1, source_target_pairs={{0,2},{1,3},{2,0},{3,1},{16,18},{17,19},{18,16},{19,17},{4,6},{5,7... | collective-permute-start | bytes 172040 | tf_op jit(solution)/shard_map/ppermute | solution.py:42
  18.1 1.5 %collective-permute-start.7 = (bf16[112,256]{1,0:T(8,128)(2,1)S(1)}, bf16[112,256]{1,0:T(8,128)(2,1)S(1)}, u32[]{:S(2)}, u32[]{:S(2)}) collective-permute-start(bf16[112,256]{1,0:T(8,128)(2,1)S(1)} %get-tuple-element.49), channel_id=1, source_target_pairs={{0,16},{1,17},{2,18},{3,19},{16,0},{17,1},{18,2},{19,3},{4,20},{5,... | collective-permute-start | bytes 172040 | tf_op jit(solution)/shard_map/ppermute | solution.py:42
  19.6 0.3 collective-permute-start.8
  19.9 0.7 %collective-permute-done.6.refs_0_ = bf16[112,256]{1,0:T(8,128)(2,1)S(1)} collective-permute-done((bf16[112,256]{1,0:T(8,128)(2,1)S(1)}, bf16[112,256]{1,0:T(8,128)(2,1)S(1)}, u32[]{:S(2)}, u32[]{:S(2)}) %collective-permute-start.6) | collective-permute-done | bytes 57376 | tf_op jit(solution)/shard_map/ppermute | solution.py:42
  20.6 1.7 %collective-permute-done.7.refs_1_ = bf16[112,256]{1,0:T(8,128)(2,1)S(1)} collective-permute-done((bf16[112,256]{1,0:T(8,128)(2,1)S(1)}, bf16[112,256]{1,0:T(8,128)(2,1)S(1)}, u32[]{:S(2)}, u32[]{:S(2)}) %collective-permute-start.7) | collective-permute-done | bytes 57376 | tf_op jit(solution)/shard_map/ppermute | solution.py:42
  22.2 2.4 %collective-permute-done.8.refs_2_ = bf16[112,256]{1,0:T(8,128)(2,1)S(1)} collective-permute-done((bf16[112,256]{1,0:T(8,128)(2,1)S(1)}, bf16[112,256]{1,0:T(8,128)(2,1)S(1)}, u32[]{:S(2)}, u32[]{:S(2)}) %collective-permute-start.8) | collective-permute-done | bytes 57376 | tf_op jit(solution)/shard_map/ppermute | solution.py:42
  24.7 0.1 collective-permute-start.9
  24.7 0.0 copy-done.2
  24.7 0.0 copy-done.4
  24.8 0.0 copy-done.5
  24.8 0.0 copy-done.6
  24.8 0.6 %rope.1 = (bf16[48,64]{1,0:T(8,128)(2,1)S(1)}, bf16[24,576]{1,0:T(8,128)(2,1)S(1)}, f32[48,512]{1,0:T(8,128)S(1)}) custom-call(bf16[48,256]{1,0:T(8,128)(2,1)S(1)} %get-tuple-element.34.after.refs_1_, bf16[24,1536]{1,0:T(8,128)(2,1)S(1)} %bitcast.15, bf16[1536,128]{1,0:T(8,128)(2,1)S(1)} %copy-done.2, bf16[24,576]{1,0:T(8,128)(2,1)S(1)} %bitcast.16, ...), custom_call_target="tpu_custom_call" | custom-call | tf_op jit(solution)/shard_map/rope/pallas_call | solution.py:213
  25.4 0.7 %collective-permute-done.9.pair_got = bf16[280,256]{1,0:T(8,128)(2,1)S(1)} collective-permute-done((bf16[280,256]{1,0:T(8,128)(2,1)S(1)}, bf16[280,256]{1,0:T(8,128)(2,1)S(1)}, u32[]{:S(2)}, u32[]{:S(2)}) %collective-permute-start.9) | collective-permute-done | bytes 143392 | tf_op jit(solution)/shard_map/ppermute | solution.py:42
  26.1 0.0 copy-done.3
  26.1 2.3 %attend.1.head_values = bf16[24,256]{1,0:T(8,128)(2,1)S(1)} custom-call(f32[24,256]{1,0:T(8,128)S(1)} %get-tuple-element.51.query_sum, bf16[280,256]{1,0:T(8,128)(2,1)S(1)} %get-tuple-element.52.pair_own, bf16[280,256]{1,0:T(8,128)(2,1)S(1)} %collective-permute-done.9.pair_got, bf16[48,64]{1,0:T(8,128)(2,1)S(1)} %get-tuple-element.53.query_rope, ...), custom_call_target="tpu_custom_call" | custom-call | tf_op jit(solution)/shard_map/attend/pallas_call | solution.py:408
  28.4 0.3 project.5
  28.7 0.3 project.6
  29.0 0.3 project.7
  29.3 1.6 %collective-permute-start.10 = (bf16[24,1792]{1,0:T(8,128)(2,1)S(1)}, bf16[24,1792]{1,0:T(8,128)(2,1)S(1)}, u32[]{:S(2)}, u32[]{:S(2)}) collective-permute-start(bf16[24,1792]{1,0:T(8,128)(2,1)S(1)} %project.5), channel_id=1, source_target_pairs={{0,4},{4,0},{8,12},{12,8},{1,5},{5,1},{9,13},{13,9},{2,6},{6,2},{1... | collective-permute-start | bytes 258056 | tf_op jit(solution)/shard_map/ppermute | solution.py:42
  30.9 2.6 %collective-permute-start.11 = (bf16[24,1792]{1,0:T(8,128)(2,1)S(1)}, bf16[24,1792]{1,0:T(8,128)(2,1)S(1)}, u32[]{:S(2)}, u32[]{:S(2)}) collective-permute-start(bf16[24,1792]{1,0:T(8,128)(2,1)S(1)} %project.6), channel_id=1, source_target_pairs={{0,8},{4,12},{8,0},{12,4},{1,9},{5,13},{9,1},{13,5},{2,10},{6,14},... | collective-permute-start | bytes 258056 | tf_op jit(solution)/shard_map/ppermute | solution.py:42
  33.5 0.2 collective-permute-start.12
  33.7 0.7 %copy.22 = f32[192,256]{1,0:T(8,128)} copy(f32[192,256]{1,0:T(8,128)S(1)} %get-tuple-element.57) | data formatting | bytes 393216
  34.3 0.7 %copy.24 = f32[192,256]{1,0:T(8,128)} copy(f32[192,256]{1,0:T(8,128)S(1)} %get-tuple-element.59) | data formatting | bytes 393216
  35.0 0.7 %copy.25 = f32[192,256]{1,0:T(8,128)} copy(f32[192,256]{1,0:T(8,128)S(1)} %get-tuple-element.60) | data formatting | bytes 393216
  35.7 0.6 %copy.23 = f32[64,256]{1,0:T(8,128)} copy(f32[64,256]{1,0:T(8,128)S(1)} %get-tuple-element.58) | data formatting | bytes 131072
  36.3 0.6 %copy.26 = f32[64,256]{1,0:T(8,128)} copy(f32[64,256]{1,0:T(8,128)S(1)} %get-tuple-element.61) | data formatting | bytes 131072
  37.0 0.6 %copy.27 = f32[64,256]{1,0:T(8,128)} copy(f32[64,256]{1,0:T(8,128)S(1)} %get-tuple-element.62) | data formatting | bytes 131072
  37.6 0.3 project.4
  37.9 0.0 collective-permute-done.10
  37.9 2.8 %collective-permute-done.11 = bf16[24,1792]{1,0:T(8,128)(2,1)S(1)} collective-permute-done((bf16[24,1792]{1,0:T(8,128)(2,1)S(1)}, bf16[24,1792]{1,0:T(8,128)(2,1)S(1)}, u32[]{:S(2)}, u32[]{:S(2)}) %collective-permute-start.11) | collective-permute-done | bytes 86048 | tf_op jit(solution)/shard_map/ppermute | solution.py:42
  40.6 0.0 collective-permute-done.12
  40.6 0.7 %fusion = bf16[1792,24]{0,1:T(8,128)(2,1)} fusion(bf16[24,1792]{1,0:T(8,128)(2,1)S(1)} %collective-permute-done.12, bf16[24,1792]{1,0:T(8,128)(2,1)S(1)} %collective-permute-done.11, f32[24,1792]{1,0:T(8,128)S(1)} %project.4, bf16[24,1792]{1,0:T(8,128)(2,1)S(1)} %collective-permute-done.10), kind=kLoop, calls=%fused_computation.1 | loop fusion | flops 301056 | bytes 516096 | tf_op jit(solution)/shard_map/transpose | solution.py:517
  (6 shorter events, 0.0 us)
Async XLA Ops:
  0.6 7.8 %copy-start.1 = (bf16[8,512,576]{1,2,0:T(8,128)(2,1)S(1)}, bf16[8,512,576]{1,2,0:T(8,128)(2,1)}, u32[]{:S(2)}) copy-start(bf16[8,512,576]{1,2,0:T(8,128)(2,1)} %param.17) | copy-start | bytes 14155780
  0.6 3.2 %collective-permute-start = (bf16[1536,256]{1,0:T(8,128)(2,1)}, bf16[1536,256]{1,0:T(8,128)(2,1)S(1)}, u32[]{:S(2)}, u32[]{:S(2)}) collective-permute-start(bf16[1536,256]{1,0:T(8,128)(2,1)} %query_own.1), channel_id=1, source_target_pairs={{0,1},{1,0},{2,3},{3,2},{16,17},{17,16},{18,19},{19,18},{4,5},{5,4... | collective-permute-start | bytes 2359304 | tf_op jit(solution)/shard_map/ppermute | solution.py:42
  1.2 2.6 %collective-permute-start.1 = (bf16[512,256]{1,0:T(8,128)(2,1)}, bf16[512,256]{1,0:T(8,128)(2,1)S(1)}, u32[]{:S(2)}, u32[]{:S(2)}) collective-permute-start(bf16[512,256]{1,0:T(8,128)(2,1)} %key_own.1), channel_id=1, source_target_pairs={{0,1},{1,0},{2,3},{3,2},{16,17},{17,16},{18,19},{19,18},{4,5},{5,4... | collective-permute-start | bytes 786440 | tf_op jit(solution)/shard_map/ppermute | solution.py:42
  1.3 2.5 %collective-permute-start.2 = (bf16[24,1536]{1,0:T(8,128)(2,1)}, bf16[24,1536]{1,0:T(8,128)(2,1)S(1)}, u32[]{:S(2)}, u32[]{:S(2)}) collective-permute-start(bf16[24,1536]{1,0:T(8,128)(2,1)} %bitcast.13), channel_id=1, source_target_pairs={{0,1},{1,0},{2,3},{3,2},{16,17},{17,16},{18,19},{19,18},{4,5},{5,4... | collective-permute-start | bytes 221192 | tf_op jit(solution)/shard_map/ppermute | solution.py:42
  4.0 7.3 %collective-permute-start.3 = (bf16[304,256]{1,0:T(8,128)(2,1)S(1)}, bf16[304,256]{1,0:T(8,128)(2,1)S(1)}, u32[]{:S(2)}, u32[]{:S(2)}) collective-permute-start(bf16[304,256]{1,0:T(8,128)(2,1)S(1)} %get-tuple-element.37), channel_id=1, source_target_pairs={{0,2},{1,3},{2,0},{3,1},{16,18},{17,19},{18,16},{19,17},{4,6},{5,7... | collective-permute-start | bytes 466952 | tf_op jit(solution)/shard_map/ppermute | solution.py:42
  6.9 6.9 %collective-permute-start.4 = (bf16[304,256]{1,0:T(8,128)(2,1)S(1)}, bf16[304,256]{1,0:T(8,128)(2,1)S(1)}, u32[]{:S(2)}, u32[]{:S(2)}) collective-permute-start(bf16[304,256]{1,0:T(8,128)(2,1)S(1)} %get-tuple-element.38), channel_id=1, source_target_pairs={{0,16},{1,17},{2,18},{3,19},{16,0},{17,1},{18,2},{19,3},{4,20},{5,... | collective-permute-start | bytes 466952 | tf_op jit(solution)/shard_map/ppermute | solution.py:42
  8.4 7.4 %collective-permute-start.5 = (bf16[304,256]{1,0:T(8,128)(2,1)S(1)}, bf16[304,256]{1,0:T(8,128)(2,1)S(1)}, u32[]{:S(2)}, u32[]{:S(2)}) collective-permute-start(bf16[304,256]{1,0:T(8,128)(2,1)S(1)} %get-tuple-element.39), channel_id=1, source_target_pairs={{0,18},{1,19},{2,16},{3,17},{16,2},{17,3},{18,0},{19,1},{4,22},{5,... | collective-permute-start | bytes 466952 | tf_op jit(solution)/shard_map/ppermute | solution.py:42
  8.5 7.4 %copy-start.7 = (f32[192,256]{1,0:T(8,128)S(1)}, f32[192,256]{1,0:T(8,128)}, u32[]{:S(2)}) copy-start(f32[192,256]{1,0:T(8,128)} %refs_5_.1) | copy-start | bytes 589828
  8.5 7.4 %copy-start.8 = (f32[192,256]{1,0:T(8,128)S(1)}, f32[192,256]{1,0:T(8,128)}, u32[]{:S(2)}) copy-start(f32[192,256]{1,0:T(8,128)} %refs_6_.1) | copy-start | bytes 589828
  8.5 7.4 %copy-start.9 = (f32[192,256]{1,0:T(8,128)S(1)}, f32[192,256]{1,0:T(8,128)}, u32[]{:S(2)}) copy-start(f32[192,256]{1,0:T(8,128)} %refs_7_.1) | copy-start | bytes 589828
  8.5 7.4 %copy-start.10 = (f32[64,256]{1,0:T(8,128)S(1)}, f32[64,256]{1,0:T(8,128)}, u32[]{:S(2)}) copy-start(f32[64,256]{1,0:T(8,128)} %refs_8_.1) | copy-start | bytes 196612
  8.5 7.4 %copy-start.11 = (f32[64,256]{1,0:T(8,128)S(1)}, f32[64,256]{1,0:T(8,128)}, u32[]{:S(2)}) copy-start(f32[64,256]{1,0:T(8,128)} %refs_9_.1) | copy-start | bytes 196612
  8.5 7.4 %copy-start.12 = (f32[64,256]{1,0:T(8,128)S(1)}, f32[64,256]{1,0:T(8,128)}, u32[]{:S(2)}) copy-start(f32[64,256]{1,0:T(8,128)} %refs_10_.1) | copy-start | bytes 196612
  15.9 8.8 %copy-start.2 = (bf16[1536,128]{1,0:T(8,128)(2,1)S(1)}, bf16[1536,128]{1,0:T(8,128)(2,1)}, u32[]{:S(2)}) copy-start(bf16[1536,128]{1,0:T(8,128)(2,1)} %weight.5) | copy-start | bytes 1179652
  15.9 8.8 %copy-start.4 = (bf16[8,3,1536]{2,0,1:T(8,128)(2,1)S(1)}, bf16[8,3,1536]{2,0,1:T(8,128)(2,1)}, u32[]{:S(2)}) copy-start(bf16[8,3,1536]{2,0,1:T(8,128)(2,1)} %param.15) | copy-start | bytes 221188
  15.9 8.8 %copy-start.5 = (bf16[8,3,576]{2,0,1:T(8,128)(2,1)S(1)}, bf16[8,3,576]{2,0,1:T(8,128)(2,1)}, u32[]{:S(2)}) copy-start(bf16[8,3,576]{2,0,1:T(8,128)(2,1)} %param.16) | copy-start | bytes 82948
  15.9 8.8 %copy-start.6 = (s32[8]{0:T(128)S(1)}, s32[8]{0:T(128)}, u32[]{:S(2)}) copy-start(s32[8]{0:T(128)} %param.18) | copy-start | bytes 100
  16.3 9.8 %copy-start.3 = (bf16[512,256]{1,0:T(8,128)(2,1)S(1)}, bf16[512,256]{1,0:T(8,128)(2,1)}, u32[]{:S(2)}) copy-start(bf16[512,256]{1,0:T(8,128)(2,1)} %value_up.1) | copy-start | bytes 786436
  16.3 4.2 %collective-permute-start.6 = (bf16[112,256]{1,0:T(8,128)(2,1)S(1)}, bf16[112,256]{1,0:T(8,128)(2,1)S(1)}, u32[]{:S(2)}, u32[]{:S(2)}) collective-permute-start(bf16[112,256]{1,0:T(8,128)(2,1)S(1)} %get-tuple-element.48), channel_id=1, source_target_pairs={{0,2},{1,3},{2,0},{3,1},{16,18},{17,19},{18,16},{19,17},{4,6},{5,7... | collective-permute-start | bytes 172040 | tf_op jit(solution)/shard_map/ppermute | solution.py:42
  18.1 4.2 %collective-permute-start.7 = (bf16[112,256]{1,0:T(8,128)(2,1)S(1)}, bf16[112,256]{1,0:T(8,128)(2,1)S(1)}, u32[]{:S(2)}, u32[]{:S(2)}) collective-permute-start(bf16[112,256]{1,0:T(8,128)(2,1)S(1)} %get-tuple-element.49), channel_id=1, source_target_pairs={{0,16},{1,17},{2,18},{3,19},{16,0},{17,1},{18,2},{19,3},{4,20},{5,... | collective-permute-start | bytes 172040 | tf_op jit(solution)/shard_map/ppermute | solution.py:42
  19.6 5.1 %collective-permute-start.8 = (bf16[112,256]{1,0:T(8,128)(2,1)S(1)}, bf16[112,256]{1,0:T(8,128)(2,1)S(1)}, u32[]{:S(2)}, u32[]{:S(2)}) collective-permute-start(bf16[112,256]{1,0:T(8,128)(2,1)S(1)} %get-tuple-element.50), channel_id=1, source_target_pairs={{0,18},{1,19},{2,16},{3,17},{16,2},{17,3},{18,0},{19,1},{4,22},{5,... | collective-permute-start | bytes 172040 | tf_op jit(solution)/shard_map/ppermute | solution.py:42
  24.7 1.4 %collective-permute-start.9 = (bf16[280,256]{1,0:T(8,128)(2,1)S(1)}, bf16[280,256]{1,0:T(8,128)(2,1)S(1)}, u32[]{:S(2)}, u32[]{:S(2)}) collective-permute-start(bf16[280,256]{1,0:T(8,128)(2,1)S(1)} %get-tuple-element.52.pair_own), channel_id=1, source_target_pairs={{0,1},{1,0},{2,3},{3,2},{16,17},{17,16},{18,19},{19,18},{4,5},{5,4... | collective-permute-start | bytes 430088 | tf_op jit(solution)/shard_map/ppermute | solution.py:42
  26.1 2.3 %copy-start = (bf16[256,7168]{1,0:T(8,128)(2,1)S(1)}, bf16[256,7168]{1,0:T(8,128)(2,1)}, u32[]{:S(2)}) copy-start(bf16[256,7168]{1,0:T(8,128)(2,1)} %weight.9) | copy-start | bytes 11010052
  29.3 8.6 %collective-permute-start.10 = (bf16[24,1792]{1,0:T(8,128)(2,1)S(1)}, bf16[24,1792]{1,0:T(8,128)(2,1)S(1)}, u32[]{:S(2)}, u32[]{:S(2)}) collective-permute-start(bf16[24,1792]{1,0:T(8,128)(2,1)S(1)} %project.5), channel_id=1, source_target_pairs={{0,4},{4,0},{8,12},{12,8},{1,5},{5,1},{9,13},{13,9},{2,6},{6,2},{1... | collective-permute-start | bytes 258056 | tf_op jit(solution)/shard_map/ppermute | solution.py:42
  30.9 9.8 %collective-permute-start.11 = (bf16[24,1792]{1,0:T(8,128)(2,1)S(1)}, bf16[24,1792]{1,0:T(8,128)(2,1)S(1)}, u32[]{:S(2)}, u32[]{:S(2)}) collective-permute-start(bf16[24,1792]{1,0:T(8,128)(2,1)S(1)} %project.6), channel_id=1, source_target_pairs={{0,8},{4,12},{8,0},{12,4},{1,9},{5,13},{9,1},{13,5},{2,10},{6,14},... | collective-permute-start | bytes 258056 | tf_op jit(solution)/shard_map/ppermute | solution.py:42
  33.5 7.2 %collective-permute-start.12 = (bf16[24,1792]{1,0:T(8,128)(2,1)S(1)}, bf16[24,1792]{1,0:T(8,128)(2,1)S(1)}, u32[]{:S(2)}, u32[]{:S(2)}) collective-permute-start(bf16[24,1792]{1,0:T(8,128)(2,1)S(1)} %project.7), channel_id=1, source_target_pairs={{0,12},{4,8},{8,4},{12,0},{1,13},{5,9},{9,5},{13,1},{2,14},{6,10},... | collective-permute-start | bytes 258056 | tf_op jit(solution)/shard_map/ppermute | solution.py:42
